TPU v7x, 16 devices: a 4x2x1 block of a 4x4x8 slice. The times are simulated.
16 devices in a mesh: data: 2 (over y, z), seq: 8 (over x, core).
Axes of the slice: x: 4, y: 2, z: 1, core: 2. Of those that a mesh axis runs over, the one named last changes fastest.
The devices are a block of a 4x4x8 slice.
Arguments:
- tokens: bfloat16 [32, 4096, 1280], P('data', 'seq'), parts along dimension 0
- lengths: int32 [32], P('data'), parts along dimension 0
- slot_params: bfloat16 [1280, 128], replicated
- logit_scale: float32 [1], replicated
- w_in: bfloat16 [32, 1280, 5120], P('seq')
- w_out: bfloat16 [32, 5120, 1280], P('seq')
Outputs:
- output: bfloat16 [32, 4096, 1280], P('data', 'seq'), parts along dimension 0
There are 2 independent parts. A program takes and returns all parts, laid end to end along the dimension named above; an argument that names none is the same for every part.
All inputs are finite; a program needn't handle non-finite values.
Results may differ from a plain program's by a relative error of at most 0.0155195.
Values are sent between devices in bfloat16 or wider.
A program may use at most 768 MiB of HBM per device.

v0:
```python
import jax
import jax.numpy as jnp
from jax import lax
from jax.sharding import PartitionSpec as P


def solution(mesh):
    seq_size = mesh.shape["seq"]

    def shard_body(tok_blk, len_blk, slot_params, logit_scale, w_in_blk, w_out_blk):
        num_rows, tok_count, model_width = tok_blk.shape
        num_slots = slot_params.shape[1]
        own_slots = num_slots // seq_size
        local_experts = w_in_blk.shape[0]
        slots_per = own_slots // local_experts
        shard_idx = lax.axis_index("seq")
        params_f32 = slot_params.astype(jnp.float32)
        col_inv = lax.rsqrt(jnp.sum(params_f32 * params_f32, axis=0, keepdims=True) + 1e-6)
        phi_norm = (params_f32 * (logit_scale[0] * col_inv)).astype(jnp.bfloat16)
        tok_f32 = tok_blk.astype(jnp.float32)
        tok_norm = (tok_f32 * lax.rsqrt(jnp.sum(tok_f32 * tok_f32, axis=-1, keepdims=True) + 1e-6)).astype(jnp.bfloat16)
        logits = jnp.einsum("btd,dn->btn", tok_norm, phi_norm, preferred_element_type=jnp.float32)
        positions = shard_idx * tok_count + jnp.arange(tok_count)
        is_valid = (positions[None, :] < len_blk[:, None])[:, :, None]
        local_max = jnp.max(jnp.where(is_valid, logits, -jnp.inf), axis=1)
        col_max = lax.pmax(local_max, "seq")
        disp_w = jnp.where(is_valid, jnp.exp(logits - col_max[:, None, :]), 0.0)
        col_sum = lax.psum(jnp.sum(disp_w, axis=1), "seq")
        part_sum = jnp.einsum("btn,btd->bnd", disp_w.astype(jnp.bfloat16), tok_blk, preferred_element_type=jnp.float32).astype(jnp.bfloat16)
        slot_sum = lax.psum_scatter(part_sum, "seq", scatter_dimension=1, tiled=True)
        own_sum = lax.dynamic_slice_in_dim(col_sum, shard_idx * own_slots, own_slots, axis=1)
        slot_in = (slot_sum.astype(jnp.float32) / own_sum[:, :, None]).astype(jnp.bfloat16)
        slot_in = slot_in.reshape(num_rows, local_experts, slots_per, model_width)
        hidden = jax.nn.gelu(jnp.einsum("besd,edf->besf", slot_in, w_in_blk, preferred_element_type=jnp.float32)).astype(jnp.bfloat16)
        slot_out = jnp.einsum("besf,efd->besd", hidden, w_out_blk, preferred_element_type=jnp.float32).astype(jnp.bfloat16)
        slot_out = slot_out.reshape(num_rows, own_slots, model_width)
        all_out = lax.all_gather(slot_out, "seq", axis=1, tiled=True)
        combine_w = jax.nn.softmax(logits, axis=-1).astype(jnp.bfloat16)
        mixed = jnp.einsum("btn,bnd->btd", combine_w, all_out, preferred_element_type=jnp.float32).astype(jnp.bfloat16)
        return jnp.where(is_valid, mixed, jnp.zeros_like(mixed))

    return jax.shard_map(
        shard_body,
        mesh=mesh,
        in_specs=(P("data", "seq", None), P("data"), P(None, None), P(None), P("seq", None, None), P("seq", None, None)),
        out_specs=P("data", "seq", None),
        check_vma=False,
    )
```

profile of v0, /device:TPU:113, one launch (start us, length us, event | category | flops | bytes accessed | tf_op | source)
XLA Modules:
  0.0 196.7 jit_solution(5752797008860832883)
XLA Ops:
  6.5 0.0 reduce-scatter.2.cloned.1.call-start
  7.2 0.0 copy-start.1
  7.2 1.2 fusion.38
  8.4 0.0 copy-start.2
  8.5 0.0 copy-start
  8.5 9.9 %fusion.5 = f32[16,512]{1,0:T(8,128)S(1)} fusion(bf16[16,512,1280]{2,1,0:T(8,128)(2,1)} %param.6), kind=kLoop, calls=%fused_computation.7 | loop fusion | flops 31449088 | bytes 21004288 | tf_op jit(solution)/shard_map/reduce_sum | solution.py:21
  18.4 0.0 copy-done.2
  18.4 0.1 broadcast_compare_fusion
  18.5 0.0 copy-done.1
  18.5 3.3 %copy-done = bf16[16,512,1280]{2,1,0:T(8,128)(2,1)S(1)} copy-done((bf16[16,512,1280]{2,1,0:T(8,128)(2,1)S(1)}, bf16[16,512,1280]{2,1,0:T(8,128)(2,1)}, u32[]{:S(2)}) %copy-start) | copy-done | bytes 20971544
  21.7 7.7 %select_reduce_fusion = (f32[16,128]{1,0:T(8,128)S(1)}, f32[16,512,128]{2,1,0:T(8,128)}) fusion(pred[16,512]{1,0:T(8,128)(4,1)S(1)} %broadcast_compare_fusion, bf16[1280,128]{1,0:T(8,128)(2,1)S(1)} %copy-done.1, f32[128]{0:T(128)S(1)} %rsqrt_multiply_fusion, bf16[16,512,1280]{2,1,0:T(8,128)(2,1)S(1)} %copy-done, f32[16,512]{1,0:T(8,128)S(1)} %add_rsqrt_fusion), kind=kOutput, calls=%fused_computation.24 | convolution fusion | flops 2718398464 | bytes 25543168 | tf_op jit(solution)/shard_map/btd,dn->btn/dot_general | solution.py:22
  29.4 13.8 %pmax.7 = f32[16,128]{1,0:T(8,128)S(1)} all-reduce(f32[16,128]{1,0:T(8,128)S(1)} %get-tuple-element.5), channel_id=1, replica_groups=mesh['data'=2,'seq'=8] {'seq'}, use_global_device_ids=true, to_apply=%region_5.6 | all-reduce | flops 2048 | bytes 16384 | tf_op jit(solution)/shard_map/pmax | solution.py:26
  43.2 12.7 %convolution_convert_fusion = bf16[16,128,1280]{2,1,0:T(8,128)(2,1)} fusion(bf16[16,512,1280]{2,1,0:T(8,128)(2,1)} %param.6, f32[16,512,128]{2,1,0:T(8,128)} %get-tuple-element.6, f32[16,128]{1,0:T(8,128)S(1)} %pmax.7, pred[16,512]{1,0:T(8,128)(4,1)S(1)} %broadcast_compare_fusion), kind=kOutput, calls=%fused_computation.14 | convolution fusion | flops 2690121728 | bytes 30425088 | tf_op jit(solution)/shard_map/btn,btd->bnd/dot_general | solution.py:29
  55.9 0.1 reduce-scatter.2.cloned.1.call-update
  56.0 0.1 all-gather.2.cloned.1.call-start
  56.0 3.6 %fusion.21 = f32[16,128]{1,0:T(8,128)S(1)} fusion(f32[16,512,128]{2,1,0:T(8,128)} %get-tuple-element.6, f32[16,128]{1,0:T(8,128)S(1)} %pmax.7, pred[16,512]{1,0:T(8,128)(4,1)S(1)} %broadcast_compare_fusion), kind=kLoop, calls=%fused_computation.27 | loop fusion | flops 3143680 | bytes 4218880 | tf_op jit(solution)/shard_map/reduce_sum | solution.py:28
  59.7 15.5 %psum.7 = f32[16,128]{1,0:T(8,128)S(1)} all-reduce(f32[16,128]{1,0:T(8,128)S(1)} %fusion.21), channel_id=1, replica_groups=mesh['data'=2,'seq'=8] {'seq'}, use_global_device_ids=true, to_apply=%region_8.9 | all-reduce | flops 2048 | bytes 16384 | tf_op jit(solution)/shard_map/psum | solution.py:28
  75.1 0.1 constant_dynamic-slice_fusion
  75.2 16.3 %reduce-scatter.2.cloned.1.call-done = bf16[16,16,1280]{2,1,0:T(8,128)(2,1)} async-done(((bf16[16,128,1280]{2,1,0:T(8,128)(2,1)}), bf16[16,16,1280]{2,1,0:T(8,128)(2,1)}) %reduce-scatter.2.cloned.1.call-update) | async-done | bytes 655376 | tf_op jit(solution)/shard_map/reduce_scatter | solution.py:30
  91.5 1.4 divide_convert_fusion.2
  92.9 0.2 copy.13
  93.1 18.6 %fusion.10 = f32[16,4,4,5120]{3,0,2,1:T(8,128)S(1)} fusion(bf16[16,4,4,1280]{3,0,2,1:T(8,128)(2,1)S(1)} %bitcast.32, bf16[4,1280,5120]{2,1,0:T(8,128)(2,1)} %param.10), kind=kOutput, calls=%fused_computation.13 | convolution fusion | flops 3355443200 | bytes 58327040 | tf_op jit(solution)/shard_map/besd,edf->besf/dot_general | solution.py:34
  111.7 18.7 %fusion.28 = bf16[4,16,4,1280]{3,1,2,0:T(8,128)(2,1)S(1)} fusion(bf16[4,5120,1280]{2,1,0:T(8,128)(2,1)} %param.11, f32[16,4,4,5120]{3,0,2,1:T(8,128)S(1)} %fusion.10), kind=kOutput, calls=%fused_computation.33 | convolution fusion | flops 3367567360 | bytes 58327040 | tf_op jit(solution)/shard_map/besf,efd->besd/dot_general | solution.py:35
  130.4 1.0 copy.9
  131.4 0.1 all-gather.2.cloned.1.call-update
  131.5 5.7 %fusion.49 = f32[16,512]{1,0:T(8,128)S(1)} fusion(f32[16,512,128]{2,1,0:T(8,128)} %get-tuple-element.6), kind=kOutput, calls=%fused_computation.56 | output fusion | flops 2097279 | bytes 4227072 | tf_op jit(solution)/shard_map/sub | solution.py:38
  137.2 28.8 %all-gather.2.cloned.1.call-done = bf16[16,128,1280]{2,1,0:T(8,128)(2,1)} async-done(((bf16[16,16,1280]{2,1,0:T(8,128)(2,1)}), bf16[16,128,1280]{2,1,0:T(8,128)(2,1)}) %all-gather.2.cloned.1.call-update) | async-done | bytes 5242896 | tf_op jit(solution)/shard_map/all_gather | solution.py:37
  166.0 23.8 %convert_select_fusion = bf16[16,512,1280]{2,1,0:T(8,128)(2,1)} fusion(pred[16,512]{1,0:T(8,128)(4,1)S(1)} %broadcast_compare_fusion, bf16[16,128,1280]{2,1,0:T(8,128)(2,1)} %all-gather.2.cloned.1.call-done, f32[16,512]{1,0:T(8,128)S(1)} %fusion.49, f32[16,512,128]{2,1,0:T(8,128)} %get-tuple-element.6), kind=kOutput, calls=%fused_computation.10 | convolution fusion | flops 2708480000 | bytes 30449664 | tf_op jit(solution)/shard_map/btn,bnd->btd/dot_general | solution.py:39
  (3 shorter events, 0.0 us)
Async XLA Ops:
  6.5 85.0 %reduce-scatter.2.cloned.1.call-start = ((), (), s32[]{:S(2)}) async-start(), calls=%async_computation.1 | async-start | bytes 5898240 | tf_op jit(solution)/shard_map/reduce_scatter | solution.py:30
  7.2 11.3 %copy-start.1 = (bf16[1280,128]{1,0:T(8,128)(2,1)S(1)}, bf16[1280,128]{1,0:T(8,128)(2,1)}, u32[]{:S(2)}) copy-start(bf16[1280,128]{1,0:T(8,128)(2,1)} %param.8) | copy-start | bytes 983044
  8.4 9.9 %copy-start.2 = (s32[16]{0:T(128)S(1)}, s32[16]{0:T(128)}, u32[]{:S(2)}) copy-start(s32[16]{0:T(128)} %param.7) | copy-start | bytes 196
  8.5 13.3 %copy-start = (bf16[16,512,1280]{2,1,0:T(8,128)(2,1)S(1)}, bf16[16,512,1280]{2,1,0:T(8,128)(2,1)}, u32[]{:S(2)}) copy-start(bf16[16,512,1280]{2,1,0:T(8,128)(2,1)} %param.6) | copy-start | bytes 62914564
  56.0 110.0 %all-gather.2.cloned.1.call-start = ((), (), s32[]{:S(2)}) async-start(), calls=%async_computation.2 | async-start | bytes 5898240 | tf_op jit(solution)/shard_map/all_gather | solution.py:37
Sparse Core Ops, SparseCore 0:
  56.1 35.3 reduce-scatter.1
  131.6 34.3 all-gather.1
where the time goes:
time: 197 us
  matrix products  81.5 us (41%)
  waiting for transfers between devices  45.1 us (23%)
  blocking collectives  29.2 us (15%)
  other arithmetic  21.9 us (11%)
  between operations  14.2 us (7%)
  local copies, waits for them, and re-layouts  4.6 us (2%)
    all_gather x1, waiting for transfers between devices, shard_body(): all_out = lax.all_gather(slot_out, 'seq', axis=1, tiled=True)  28.8 us
    dot_general x1, matrix products, shard_body(): jnp.einsum('btn,bnd->btd', combine_w, all_out, preferred_element_type=jnp...  23.8 us
    dot_general x1, matrix products, shard_body(): jnp.einsum('besf,efd->besd', hidden, w_out_blk, preferred_element_type=jn...  18.7 us
    dot_general x1, matrix products, shard_body(): jnp.einsum('besd,edf->besf', slot_in, w_in_blk, preferred_element_type=jn...  18.6 us
    reduce_scatter x1, waiting for transfers between devices, shard_body(): lax.psum_scatter(part_sum, 'seq', scatter_dimension=1, tiled=True)  16.3 us
    psum x1, blocking collectives, shard_body(): col_sum = lax.psum(jnp.sum(disp_w, axis=1), 'seq')  15.5 us
    pmax x1, blocking collectives, shard_body(): col_max = lax.pmax(local_max, 'seq')  13.8 us
    dot_general x1, matrix products, shard_body(): jnp.einsum('btn,btd->bnd', disp_w.astype(jnp.bfloat16), tok_blk, preferre...  12.7 us
  transfers between devices with their start and end apart: 2, of which 2 were waited for; matrix products, arithmetic and copies ran while one was open for 5% of the time, Pallas kernels for 0%

commit v1 on v0

v1 whole, which is shorter than its diff:
```python
import functools

import jax
import jax.numpy as jnp
from jax import lax
from jax.experimental import pallas as pl
from jax.experimental.pallas import tpu as pltpu
from jax.sharding import PartitionSpec as P

MESH = pl.DeviceIdType.MESH
F32, BF16 = jnp.float32, jnp.bfloat16
TOK_SLOTS = 4
W_SLOTS = 14
F_BLOCK = 512
ROW_TILE = 128


def iota(shape, dim):
    return lax.broadcasted_iota(jnp.int32, shape, dim)


def route_kernel(
    lens, gain, phi, tok, w_in, w_out, c_out, y_out,
    tok_buf, phin, wt_buf, s_f32, c_buf, part, from_partner, relay_r, relay_l, from_l, from_r, xs, z_own, z_all,
    xk, y_acc, ys, wi_buf, wo_buf,
    tok_sem, wi_sem, wo_sem, c_sem, yo_sem, z_send, z_recv,
    d_send, d_recv, rs_send, rs_recv, ag_send, ag_recv,
):
    rows, tokens, width = tok.shape
    experts, _, ff = w_in.shape
    slots = phi.shape[1]
    pairs = rows // 2
    blocks = ff // F_BLOCK
    steps = experts * blocks
    me = lax.axis_index("seq")
    chip, core = me // 2, lax.rem(me, 2)

    def dev(chip_step, flip=0):
        other = lax.rem(chip + chip_step, 4)
        return other * 2 + (1 - core if flip else core)

    left, right, opposite, partner = dev(3), dev(1), dev(2), dev(0, 1)
    c_left, c_right, c_opp = lax.rem(chip + 3, 4), lax.rem(chip + 1, 4), lax.rem(chip + 2, 4)

    barrier = pltpu.get_barrier_semaphore()
    for step in range(1, 8):
        peer = lax.rem(me + step, 8)
        pl.semaphore_signal(barrier, inc=1, device_id={"seq": peer}, device_id_type=MESH)

    def tok_copy(b):
        slot = lax.rem(b, TOK_SLOTS)
        return pltpu.make_async_copy(tok.at[b], tok_buf.at[slot], tok_sem.at[slot])

    def w_copies(i):
        e, f, slot = i // blocks, lax.rem(i, blocks), lax.rem(i, W_SLOTS)
        cols = pl.ds(pl.multiple_of(f * F_BLOCK, F_BLOCK), F_BLOCK)
        return (
            pltpu.make_async_copy(w_in.at[e, :, cols], wi_buf.at[slot], wi_sem.at[slot]),
            pltpu.make_async_copy(w_out.at[e, cols, :], wo_buf.at[slot], wo_sem.at[slot]),
        )

    for b in range(TOK_SLOTS):
        tok_copy(b).start()

    gain_s = gain[0]
    phi_f32 = phi[...].astype(F32)
    col_inv = lax.rsqrt(jnp.sum(phi_f32 * phi_f32, axis=0, keepdims=True) + 1e-6)
    phi_n = (phi_f32 * (gain_s * col_inv)).astype(BF16)
    src, dst = iota((slots, slots), 0), iota((slots, slots), 1)
    kk, hh, cc, rest = dst // 64, (dst // 32) % 2, (dst // 8) % 4, dst % 8
    perm = (src == cc * 32 + hh * 16 + kk * 8 + rest).astype(F32).astype(BF16)
    phin[...] = jnp.dot(phi_n, perm, preferred_element_type=F32).astype(BF16)

    def one_batch(b, which):
        slot = lax.rem(b, TOK_SLOTS)
        tok_copy(b).wait()
        x_ref = tok_buf.at[slot]
        length = lens[b]
        z_row = jnp.zeros((1, slots), F32)
        for r in range(tokens // ROW_TILE):
            tile = pl.ds(r * ROW_TILE, ROW_TILE)
            x = x_ref[tile, :].astype(F32)
            inv = lax.rsqrt(jnp.sum(x * x, axis=-1, keepdims=True) + 1e-6)
            logits = jnp.dot((x * inv).astype(BF16), phin[...], preferred_element_type=F32)
            e = jnp.exp(logits - gain_s)
            pos = me * tokens + r * ROW_TILE + iota((ROW_TILE, slots), 0)
            valid = pos < length
            total = jnp.sum(e, axis=-1, keepdims=True)
            c_buf[b, tile, :] = jnp.where(valid, e / total, 0.0).astype(BF16)
            w = jnp.where(valid, e, 0.0)
            z_row += jnp.sum(w, axis=0, keepdims=True)
            wt_buf[:, tile] = w.T.astype(BF16)
        z_own[pl.ds(b, 1), :] = z_row
        s_f32[which] = jnp.dot(wt_buf[...], x_ref[...], preferred_element_type=F32)

        @pl.when(b + TOK_SLOTS < rows)
        def _():
            tok_copy(b + TOK_SLOTS).start()

        @pl.when(b < W_SLOTS)
        def _():
            for copy in w_copies(b):
                copy.start()

    def one_pair(p, carry):
        for which in range(2):
            one_batch(2 * p + which, which)
        for g in range(16):
            eight = pl.ds(g * 8, 8)
            both = jnp.concatenate([s_f32[0, eight, :], s_f32[1, eight, :]], axis=0)
            part[g // 8, (g // 4) % 2, g % 4, p] = both.astype(BF16)
        return carry

    def remote(src_ref, dst_ref, send, recv, to):
        return pltpu.make_async_remote_copy(
            src_ref=src_ref, dst_ref=dst_ref, send_sem=send, recv_sem=recv, device_id={"seq": to}, device_id_type=MESH
        )

    def d2d(kk, q):
        two = pl.ds(2 * q, 2)
        return remote(part.at[kk, 1 - core, :, two], from_partner.at[kk, :, two], d_send.at[kk, q], d_recv.at[kk, q], partner)

    def rs_copy(kind, kk, q):
        plus, minus = 2 * q, 2 * q + 1
        mine = part.at[kk, core]
        src_ref, dst_ref, to = {
            "ap": (mine.at[c_opp, plus], relay_r.at[kk, q], right),
            "am": (mine.at[c_opp, minus], relay_l.at[kk, q], left),
            "bp0": (mine.at[c_right, minus], from_l.at[kk, minus], right),
            "bm0": (mine.at[c_left, plus], from_r.at[kk, plus], left),
            "bp1": (mine.at[c_right, plus], from_l.at[kk, plus], right),
            "bm1": (mine.at[c_left, minus], from_r.at[kk, minus], left),
        }[kind]
        n = ("ap", "am", "bp0", "bm0", "bp1", "bm1").index(kind)
        return remote(src_ref, dst_ref, rs_send.at[n, kk, q], rs_recv.at[n, kk, q], to)

    def s2(kk, q):
        d2d(kk, q).wait_recv()
        for c in range(4):
            for p in (2 * q, 2 * q + 1):
                total = part[kk, core, c, p].astype(F32) + from_partner[kk, c, p].astype(F32)
                part[kk, core, c, p] = total.astype(BF16)
        for kind in ("ap", "am", "bp0", "bm0"):
            rs_copy(kind, kk, q).start()

    def s3(kk, q):
        rs_copy("ap", kk, q).wait_recv()
        plus, minus = 2 * q, 2 * q + 1
        part[kk, core, c_right, plus] = (
            part[kk, core, c_right, plus].astype(F32) + relay_r[kk, q].astype(F32)
        ).astype(BF16)
        rs_copy("bp1", kk, q).start()
        rs_copy("am", kk, q).wait_recv()
        part[kk, core, c_left, minus] = (
            part[kk, core, c_left, minus].astype(F32) + relay_l[kk, q].astype(F32)
        ).astype(BF16)
        rs_copy("bm1", kk, q).start()

    def s4(kk):
        lane0 = kk * 64 + core * 32 + chip * 8
        pick = iota((16, slots), 1) == lane0 + iota((16, slots), 0) % 8
        for q in range(4):
            for kind in ("bp0", "bm0", "bp1", "bm1"):
                rs_copy(kind, kk, q).wait_recv()
            for p in (2 * q, 2 * q + 1):
                z = z_own[2 * p : 2 * p + 2, :]
                for step in range(1, 8):
                    z += z_all[lax.rem(me + step, 8), 2 * p : 2 * p + 2, :]
                z16 = jnp.concatenate([jnp.broadcast_to(z[i : i + 1], (8, slots)) for i in range(2)], axis=0)
                z_col = jnp.sum(jnp.where(pick, z16, 0.0), axis=1, keepdims=True)
                total = part[kk, core, chip, p].astype(F32) + from_l[kk, p].astype(F32) + from_r[kk, p].astype(F32)
                xs[kk, p] = (total / z_col).astype(BF16)

    def z_copy(step):
        peer = lax.rem(me + step, 8)
        return remote(z_own, z_all.at[me], z_send.at[step - 1], z_recv.at[step - 1], peer)

    def chunk(q):
        lax.fori_loop(2 * q, 2 * q + 2, one_pair, 0)

    chunk(0)
    pl.semaphore_wait(barrier, 7)
    for q in range(4):
        if q:
            chunk(q)
        d2d(0, q).start()
        d2d(1, q).start()
        if q >= 1:
            s2(0, q - 1)
        if q >= 2:
            s3(0, q - 2)
    for step in range(1, 8):
        z_copy(step).start()
    c_copy = pltpu.make_async_copy(c_buf, c_out, c_sem)
    c_copy.start()
    s2(0, 3)
    s3(0, 2)
    s2(1, 0)
    s3(0, 3)
    s2(1, 1)
    for step in range(1, 8):
        z_copy(step).wait_recv()
    s2(1, 2)
    s3(1, 0)
    s4(0)

    half = 2 * rows
    lo, hi = pl.ds(0, half), pl.ds(half, half)

    def ag_copy(kind, k):
        blk = ys.at[k]
        src_blk, part_rows, to = {
            "rp": (me, lo, right),
            "lm": (me, hi, left),
            "rm": (me, hi, right),
            "lp": (me, lo, left),
            "fr": (left, lo, right),
            "fl": (right, hi, left),
            "po": (me, None, partner),
            "pl": (left, None, partner),
            "pr": (right, None, partner),
            "pp": (opposite, None, partner),
        }[kind]
        n = ("rp", "lm", "rm", "lp", "fr", "fl", "po", "pl", "pr", "pp").index(kind)
        ref = blk.at[src_blk] if part_rows is None else blk.at[src_blk, part_rows]
        return remote(ref, ref, ag_send.at[n, k], ag_recv.at[n, k], to)

    def a1(k):
        for kind in ("rp", "lm", "rm", "lp", "po"):
            ag_copy(kind, k).start()

    def a2(k):
        ag_copy("rp", k).wait_recv()
        ag_copy("fr", k).start()
        ag_copy("lm", k).wait_recv()
        ag_copy("fl", k).start()

    def a3(k):
        ag_copy("rm", k).wait_recv()
        ag_copy("pl", k).start()
        ag_copy("lp", k).wait_recv()
        ag_copy("pr", k).start()

    def a4(k):
        ag_copy("fr", k).wait_recv()
        ag_copy("fl", k).wait_recv()
        ag_copy("pp", k).start()

    def y_copy(k):
        return pltpu.make_async_copy(ys.at[k], y_out.at[k], yo_sem.at[k])

    def a5(k):
        for kind in ("po", "pl", "pr", "pp"):
            ag_copy(kind, k).wait_recv()
        y_copy(k).start()

    hooks = {
        0: [lambda: s2(1, 3)],
        1: [lambda: s3(1, 1)],
        3: [lambda: s3(1, 2)],
        5: [lambda: s3(1, 3)],
        14: [lambda: a2(0)],
        17: [lambda: a3(0)],
        19: [lambda: s4(1)],
        22: [lambda: a4(0)],
        24: [lambda: a2(1)],
        26: [lambda: a5(0), lambda: a3(1)],
        32: [lambda: a4(1)],
        34: [lambda: a2(2)],
        36: [lambda: a5(1), lambda: a3(2)],
    }

    def ffn_step(i, carry):
        k, f, slot = i // blocks, lax.rem(i, blocks), lax.rem(i, W_SLOTS)

        @pl.when(f == 0)
        def _():
            k2 = lax.rem(k, 2)
            r, c = iota((4 * rows, 8 * rows), 0), iota((4 * rows, 8 * rows), 1)
            sel = (c == (r // 4) * 8 + k2 * 4 + r % 4).astype(F32).astype(BF16)
            pair = xs[k // 2].reshape(8 * rows, width)
            xk[...] = jnp.dot(sel, pair, preferred_element_type=F32).astype(BF16)
            y_acc[...] = jnp.zeros_like(y_acc)

        wi, wo = w_copies(i)
        wi.wait()
        h = jnp.dot(xk[...], wi_buf[slot], preferred_element_type=F32)
        h = jax.nn.gelu(h).astype(BF16)
        wo.wait()
        y_acc[...] += jnp.dot(h, wo_buf[slot], preferred_element_type=F32)

        @pl.when(i + W_SLOTS < steps)
        def _():
            for copy in w_copies(i + W_SLOTS):
                copy.start()

        for at, todo in hooks.items():
            @pl.when(i == at)
            def _(todo=todo):
                for hook in todo:
                    hook()

        @pl.when(f == blocks - 1)
        def _():
            ys[k, me] = y_acc[...].astype(BF16)
            a1(k)

        return carry

    lax.fori_loop(0, steps, ffn_step, 0)
    a4(2)
    a2(3)
    a5(2)
    a3(3)
    a4(3)
    a5(3)

    c_copy.wait()
    for k in range(4):
        y_copy(k).wait()
    for step in range(1, 8):
        z_copy(step).wait_send()
    for kk in range(2):
        for q in range(4):
            d2d(kk, q).wait_send()
            for kind in ("ap", "am", "bp0", "bm0", "bp1", "bm1"):
                rs_copy(kind, kk, q).wait_send()
    for k in range(4):
        for kind in ("rp", "lm", "rm", "lp", "fr", "fl", "po", "pl", "pr", "pp"):
            ag_copy(kind, k).wait_send()


def combine_kernel(c_ref, y_ref, out_ref):
    experts, devs, eight, width = y_ref.shape
    slots = c_ref.shape[2]
    r = y_ref[...].reshape(experts * devs, eight, width).astype(F32).reshape(experts * devs * eight, width).astype(BF16)
    col, row = iota((slots, 2 * slots), 0), iota((slots, 2 * slots), 1)
    kk, core, chip, k2, s = col // 64, (col // 32) % 2, (col // 8) % 4, (col // 4) % 2, col % 4
    base = (kk * 2 + k2) * 64 + (chip * 2 + core) * 8 + s
    for which in range(2):
        spread = (row == base + which * 4).astype(F32).astype(BF16)
        c = jnp.dot(c_ref[which], spread, preferred_element_type=F32).astype(BF16)
        out_ref[which] = jnp.dot(c, r, preferred_element_type=F32).astype(BF16)


def solution(mesh):
    def shard_body(tok, lens, phi, gain, w_in, w_out):
        rows, tokens, width = tok.shape
        experts, _, ff = w_in.shape
        slots = phi.shape[1]
        pairs = rows // 2
        any_spec = pl.BlockSpec(memory_space=pl.ANY)
        smem = pl.BlockSpec(memory_space=pltpu.SMEM)
        dma = pltpu.SemaphoreType.DMA
        blk = (16, width)
        c, y = pl.pallas_call(
            route_kernel,
            out_shape=(
                jax.ShapeDtypeStruct((rows, tokens, slots), BF16),
                jax.ShapeDtypeStruct((experts, 8, 4 * rows, width), BF16),
            ),
            in_specs=[smem, smem, pl.BlockSpec(memory_space=pltpu.VMEM), any_spec, any_spec, any_spec],
            out_specs=(any_spec, any_spec),
            scratch_shapes=[
                pltpu.VMEM((TOK_SLOTS, tokens, width), BF16),
                pltpu.VMEM((width, slots), BF16),
                pltpu.VMEM((slots, tokens), BF16),
                pltpu.VMEM((2, slots, width), F32),
                pltpu.VMEM((rows, tokens, slots), BF16),
                pltpu.VMEM((2, 2, 4, pairs) + blk, BF16),
                pltpu.VMEM((2, 4, pairs) + blk, BF16),
                pltpu.VMEM((2, 4) + blk, BF16),
                pltpu.VMEM((2, 4) + blk, BF16),
                pltpu.VMEM((2, pairs) + blk, BF16),
                pltpu.VMEM((2, pairs) + blk, BF16),
                pltpu.VMEM((2, pairs) + blk, BF16),
                pltpu.VMEM((rows, slots), F32),
                pltpu.VMEM((8, rows, slots), F32),
                pltpu.VMEM((4 * rows, width), BF16),
                pltpu.VMEM((4 * rows, width), F32),
                pltpu.VMEM((experts, 8, 4 * rows, width), BF16),
                pltpu.VMEM((W_SLOTS, width, F_BLOCK), BF16),
                pltpu.VMEM((W_SLOTS, F_BLOCK, width), BF16),
                dma((TOK_SLOTS,)), dma((W_SLOTS,)), dma((W_SLOTS,)), dma, dma((4,)), dma((7,)), dma((7,)),
                dma((2, 4)), dma((2, 4)), dma((6, 2, 4)), dma((6, 2, 4)), dma((10, 4)), dma((10, 4)),
            ],
            compiler_params=pltpu.CompilerParams(
                collective_id=0, has_side_effects=True, vmem_limit_bytes=67_000_000
            ),
            name="route",
        )(lens, gain, phi, tok, w_in, w_out)
        return pl.pallas_call(
            combine_kernel,
            out_shape=jax.ShapeDtypeStruct(tok.shape, BF16),
            grid=(pairs,),
            in_specs=[
                pl.BlockSpec((2, tokens, slots), lambda p: (p, 0, 0)),
                pl.BlockSpec((experts, 8, 8, width), lambda p: (0, 0, p, 0)),
            ],
            out_specs=pl.BlockSpec((2, tokens, width), lambda p: (p, 0, 0)),
            compiler_params=pltpu.CompilerParams(vmem_limit_bytes=50_000_000),
            name="combine",
        )(c, y)

    return jax.shard_map(
        shard_body,
        mesh=mesh,
        in_specs=(P("data", "seq", None), P("data"), P(None, None), P(None), P("seq", None, None), P("seq", None, None)),
        out_specs=P("data", "seq", None),
        check_vma=False,
    )
```

time: 197 us -> 100 us (0.51)
  Pallas kernels: 0 us -> 97.7 us
  matrix products: 81.5 us -> 0 us
  waiting for transfers between devices: 45.1 us -> 0 us
  blocking collectives: 29.2 us -> 0 us
  other arithmetic: 21.9 us -> 0 us
  between operations: 14.2 us -> 0.67 us
  local copies, waits for them, and re-layouts: 4.6 us -> 1.58 us
    pallas_call x0 -> x2, Pallas kernels: none -> 97.7 us  [the longest x1 84.4 us: shard_body(): pl.pallas_call(route_kernel, out_shape=(jax.ShapeDtypeStruct((rows, token...]
    dot_general x5 -> x0, matrix products: 81.5 us -> none  [the longest x1 23.8 us: shard_body(): jnp.einsum('btn,bnd->btd', combine_w, all_out, preferred_element_type=jnp...]
    all_gather x1 -> x0, waiting for transfers between devices: 28.8 us -> none  [shard_body(): all_out = lax.all_gather(slot_out, 'seq', axis=1, tiled=True)]
    reduce_scatter x1 -> x0, waiting for transfers between devices: 16.3 us -> none  [shard_body(): lax.psum_scatter(part_sum, 'seq', scatter_dimension=1, tiled=True)]
    psum x1 -> x0, blocking collectives: 15.5 us -> none  [shard_body(): col_sum = lax.psum(jnp.sum(disp_w, axis=1), 'seq')]
    reduce_sum x3 -> x0, other arithmetic: 14.7 us -> none  [the longest x1 9.86 us: shard_body(): jnp.sum(tok_f32 * tok_f32, axis=-1, keepdims=True) + 1e-06]
    pmax x1 -> x0, blocking collectives: 13.8 us -> none  [shard_body(): col_max = lax.pmax(local_max, 'seq')]
    sub x1 -> x0, other arithmetic: 5.72 us -> none  [shard_body(): combine_w = jax.nn.softmax(logits, axis=-1).astype(jnp.bfloat16)]
  transfers between devices with their start and end apart: 2 -> 0, of which waited for: 2 -> 0; matrix products, arithmetic and copies ran while one was open for 5% -> 0% of each run, Pallas kernels for 0% -> 0%
where the time goes in v1:
time: 100 us; the launch traced here: 99.9 us
  Pallas kernels  97.7 us (98%)
  local copies, waits for them, and re-layouts  1.58 us (2%)
    pallas_call x1, Pallas kernels, shard_body(): pl.pallas_call(route_kernel, out_shape=(jax.ShapeDtypeStruct((rows, token...  84.4 us
    pallas_call x1, Pallas kernels, shard_body(): pl.pallas_call(combine_kernel, out_shape=jax.ShapeDtypeStruct(tok.shape,...  13.3 us

profile of v1, /device:TPU:113, one launch (start us, length us, event | category | flops | bytes accessed | tf_op | source)
XLA Modules:
  0.0 99.9 jit_solution(1155200519931968570)
XLA Ops:
  0.7 84.4 %route.1 = (bf16[16,512,128]{2,1,0:T(8,128)(2,1)}, bf16[4,8,64,1280]{3,2,1,0:T(8,128)(2,1)}) custom-call(s32[16]{0:T(128)} %lens.1, f32[1]{0:T(128)S(6)} %copy.7.gain, bf16[1280,128]{1,0:T(8,128)(2,1)} %phi.1, bf16[16,512,1280]{2,1,0:T(8,128)(2,1)} %tok.1, bf16[4,1280,5120]{2,1,0:T(8,128)(2,1)} %w_in.1, bf16[4,5120,1280]{2,1,0:T(8,128)(2,1)} %w_out.1), custom_call_target="tpu_custom_call" | custom-call | tf_op jit(solution)/shard_map/route/pallas_call | solution.py:356
  85.1 0.0 copy-start
  85.1 1.6 %copy-done = bf16[16,512,128]{2,1,0:T(8,128)(2,1)S(1)} copy-done((bf16[16,512,128]{2,1,0:T(8,128)(2,1)S(1)}, bf16[16,512,128]{2,1,0:T(8,128)(2,1)}, u32[]{:S(2)}) %copy-start) | copy-done | bytes 2097176
  86.7 13.3 %combine.1 = bf16[16,512,1280]{2,1,0:T(8,128)(2,1)} custom-call(bf16[16,512,128]{2,1,0:T(8,128)(2,1)S(1)} %copy-done, bf16[4,8,64,1280]{3,2,1,0:T(8,128)(2,1)} %get-tuple-element.8.y_ref), custom_call_target="tpu_custom_call" | custom-call | tf_op jit(solution)/shard_map/combine/pallas_call | solution.py:392
Async XLA Ops:
  85.1 1.6 %copy-start = (bf16[16,512,128]{2,1,0:T(8,128)(2,1)S(1)}, bf16[16,512,128]{2,1,0:T(8,128)(2,1)}, u32[]{:S(2)}) copy-start(bf16[16,512,128]{2,1,0:T(8,128)(2,1)} %get-tuple-element.7.c_ref) | copy-start | bytes 6291460

commit v2 on v0

v2 whole, which is shorter than its diff:
```python
import functools

import jax
import jax.numpy as jnp
from jax import lax
from jax.experimental import pallas as pl
from jax.experimental.pallas import tpu as pltpu
from jax.sharding import PartitionSpec as P

MESH = pl.DeviceIdType.MESH
F32, BF16 = jnp.float32, jnp.bfloat16
TOK_SLOTS = 4
W_SLOTS = 6
F_BLOCK = 1280
ROW_TILE = 128


def iota(shape, dim):
    return lax.broadcasted_iota(jnp.int32, shape, dim)


def route_kernel(
    lens, gain, phi, tok, w_in, w_out, c_out, y_out,
    tok_buf, phin, wt_buf, s_f32, c_buf, part, from_partner, relay_r, relay_l, from_l, from_r, from_opp, xs, z_own, z_all, z_tot,
    xk, h_buf, y_acc, ys, wi_buf, wo_buf,
    tok_sem, wi_sem, wo_sem, c_sem, yo_sem, z_send, z_recv,
    d_send, d_recv, a_send, a_recv, b_send, b_recv, o_send, o_recv, ag_send, ag_recv,
):
    rows, tokens, width = tok.shape
    experts, _, ff = w_in.shape
    slots = phi.shape[1]
    pairs = rows // 2
    blocks = ff // F_BLOCK
    steps = experts * blocks
    me = lax.axis_index("seq")
    chip, core = me // 2, lax.rem(me, 2)

    def dev(chip_step, flip=0):
        other = lax.rem(chip + chip_step, 4)
        return other * 2 + (1 - core if flip else core)

    left, right, opposite, partner = dev(3), dev(1), dev(2), dev(0, 1)
    c_left, c_right, c_opp = lax.rem(chip + 3, 4), lax.rem(chip + 1, 4), lax.rem(chip + 2, 4)

    barrier = pltpu.get_barrier_semaphore()
    for step in range(1, 8):
        peer = lax.rem(me + step, 8)
        pl.semaphore_signal(barrier, inc=1, device_id={"seq": peer}, device_id_type=MESH)

    def tok_copy(b):
        slot = lax.rem(b, TOK_SLOTS)
        return pltpu.make_async_copy(tok.at[b], tok_buf.at[slot], tok_sem.at[slot])

    def w_copies(i):
        e, f, slot = i // blocks, lax.rem(i, blocks), lax.rem(i, W_SLOTS)
        cols = pl.ds(pl.multiple_of(f * F_BLOCK, F_BLOCK), F_BLOCK)
        return (
            pltpu.make_async_copy(w_in.at[e, :, cols], wi_buf.at[slot], wi_sem.at[slot]),
            pltpu.make_async_copy(w_out.at[e, cols, :], wo_buf.at[slot], wo_sem.at[slot]),
        )

    for b in range(TOK_SLOTS):
        tok_copy(b).start()

    gain_s = gain[0]
    phi_f32 = phi[...].astype(F32)
    col_inv = lax.rsqrt(jnp.sum(phi_f32 * phi_f32, axis=0, keepdims=True) + 1e-6)
    phi_n = (phi_f32 * (gain_s * col_inv)).astype(BF16)
    src, dst = iota((slots, slots), 0), iota((slots, slots), 1)
    kk, hh, cc, rest = dst // 64, (dst // 32) % 2, (dst // 8) % 4, dst % 8
    perm = (src == cc * 32 + hh * 16 + kk * 8 + rest).astype(F32).astype(BF16)
    phin[...] = jnp.dot(phi_n, perm, preferred_element_type=F32).astype(BF16)

    def c_copy(p):
        slot = lax.rem(p, 2)
        return pltpu.make_async_copy(c_buf.at[slot], c_out.at[pl.ds(2 * p, 2)], c_sem.at[slot])

    def pack_pair(p):
        for g in range(16):
            eight = pl.ds(g * 8, 8)
            both = jnp.concatenate([s_f32[0, eight, :], s_f32[1, eight, :]], axis=0)
            part[g // 8, (g // 4) % 2, g % 4, p] = both.astype(BF16)

    def one_pair(p):
        for which in range(2):
            b = 2 * p + which
            x_ref = tok_buf.at[lax.rem(b, TOK_SLOTS)]
            length = lens[b]
            z_row = jnp.zeros((1, slots), F32)
            for r in range(tokens // ROW_TILE):
                tile = pl.ds(r * ROW_TILE, ROW_TILE)
                x = x_ref[tile, :].astype(F32)
                inv = lax.rsqrt(jnp.sum(x * x, axis=-1, keepdims=True) + 1e-6)
                logits = jnp.dot((x * inv).astype(BF16), phin[...], preferred_element_type=F32)
                e = jnp.exp(logits - gain_s)
                pos = me * tokens + r * ROW_TILE + iota((ROW_TILE, slots), 0)
                valid = pos < length
                total = jnp.sum(e, axis=-1, keepdims=True)
                c_buf[lax.rem(p, 2), which, tile, :] = jnp.where(valid, e / total, 0.0).astype(BF16)
                w = jnp.where(valid, e, 0.0)
                z_row += jnp.sum(w, axis=0, keepdims=True)
                wt_buf[which, :, tile] = w.T.astype(BF16)
            z_own[pl.ds(b, 1), :] = z_row
            s_f32[which] = jnp.dot(wt_buf[which], x_ref[...], preferred_element_type=F32)
        pack_pair(p)

    def remote(src_ref, dst_ref, send, recv, to):
        return pltpu.make_async_remote_copy(
            src_ref=src_ref, dst_ref=dst_ref, send_sem=send, recv_sem=recv, device_id={"seq": to}, device_id_type=MESH
        )

    lo_cols, hi_cols = pl.ds(0, width // 2), pl.ds(width // 2, width // 2)

    def settle(ref, sem):
        pltpu.make_async_copy(ref, ref, sem).wait()

    def d2d(kk, p):
        return remote(part.at[kk, 1 - core, :, p], from_partner.at[kk, :, p], d_send, d_recv.at[kk, p], partner)

    def rs_copy(kind, kk, p):
        mine = part.at[kk, core]
        to_right = kind[1] == "p"
        side, to = (0, right) if to_right else (1, left)
        if kind[0] == "a":
            cols, relay = (lo_cols, relay_r) if to_right else (hi_cols, relay_l)
            return remote(mine.at[c_opp, p, :, cols], relay.at[kk, p], a_send.at[side, kk], a_recv.at[side, kk, p], to)
        cols = hi_cols if kind in ("bp0", "bm1") else lo_cols
        c, inbox = (c_right, from_l) if to_right else (c_left, from_r)
        return remote(mine.at[c, p, :, cols], inbox.at[kk, p, :, cols], b_send.at[side], b_recv.at[side, kk], to)

    def chip_sum(kk, p):
        d2d(kk, p).wait_recv()
        for c in range(4):
            total = part[kk, core, c, p].astype(F32) + from_partner[kk, c, p].astype(F32)
            part[kk, core, c, p] = total.astype(BF16)

    def s2(kk, p):
        chip_sum(kk, p)
        for kind in ("ap", "am", "bp0", "bm0"):
            rs_copy(kind, kk, p).start()

    def last_copies():
        p = pairs - 1
        mine = part.at[0, core]
        return (
            remote(mine.at[c_opp, p], from_opp, o_send, o_recv, opposite),
            remote(mine.at[c_right, p], from_l.at[0, p], b_send.at[0], b_recv.at[0, 0], right),
            remote(mine.at[c_left, p], from_r.at[0, p], b_send.at[1], b_recv.at[1, 0], left),
        )

    def s2_last():
        chip_sum(0, pairs - 1)
        for copy in last_copies():
            copy.start()

    def s3(kk, p):
        for kind, then, c, relay, cols in (
            ("ap", "bp1", c_right, relay_r, lo_cols),
            ("am", "bm1", c_left, relay_l, hi_cols),
        ):
            rs_copy(kind, kk, p).wait_recv()
            total = part[kk, core, c, p, :, cols].astype(F32) + relay[kk, p].astype(F32)
            part[kk, core, c, p, :, cols] = total.astype(BF16)
            rs_copy(then, kk, p).start()

    def s4(kk):
        lane0 = kk * 64 + core * 32 + chip * 8
        pick = iota((16, slots), 1) == lane0 + iota((16, slots), 0) % 8
        cols = []
        for p in range(pairs):
            z16 = jnp.concatenate([jnp.broadcast_to(z_tot[b : b + 1, :], (8, slots)) for b in (2 * p, 2 * p + 1)], axis=0)
            cols.append(jnp.sum(jnp.where(pick, z16, 0.0), axis=1, keepdims=True))
        settle(from_l.at[kk], b_recv.at[0, kk])
        settle(from_r.at[kk], b_recv.at[1, kk])
        if kk == 0:
            settle(from_opp, o_recv)
        for p in range(pairs):
            total = part[kk, core, chip, p].astype(F32) + from_l[kk, p].astype(F32) + from_r[kk, p].astype(F32)
            if kk == 0 and p == pairs - 1:
                total += from_opp[...].astype(F32)
            xs[kk, p] = (total / cols[p]).astype(BF16)

    def z_copy(step):
        peer = lax.rem(me + step, 8)
        return remote(z_own, z_all.at[me], z_send, z_recv, peer)

    def when(condition, *todo):
        @pl.when(condition)
        def _():
            for f, *args in todo:
                f(*args)

    def pair_step(p, carry):
        when(p >= 2, (lambda: c_copy(p - 2).wait(),))
        for which in range(2):
            tok_copy(2 * p + which).wait()
        one_pair(p)
        d2d(0, p).start()
        d2d(1, p).start()
        c_copy(p).start()
        for which in range(2):
            b = 2 * p + TOK_SLOTS + which
            when(b < rows, (lambda b=b: tok_copy(b).start(),))
        when(p < W_SLOTS, (lambda: [copy.start() for copy in w_copies(p)],))
        odd = lax.rem(p, 2)
        when(p >= 1, (s2, 0, p - 1))
        when(p >= 3, (s3, 0, p - 3))
        when((p >= 4) & (odd == 0), (s3, 1, p // 2 - 2))
        when((p >= 2) & (odd == 0), (s2, 1, p // 2 - 1))
        return carry

    pl.semaphore_wait(barrier, 7)
    lax.fori_loop(0, pairs, pair_step, 0)
    for step in range(1, 8):
        z_copy(step).start()
    s2_last()
    s3(0, pairs - 3)
    s3(0, pairs - 2)
    s3(1, pairs // 2 - 2)
    for p in range(pairs // 2 - 1, pairs):
        s2(1, p)
    settle(z_all.at[pl.ds(0, 7)], z_recv)
    z = z_own[...]
    for step in range(1, 8):
        z += z_all[lax.rem(me + step, 8)]
    z_tot[...] = z
    s4(0)

    half = 2 * rows
    lo, hi = pl.ds(0, half), pl.ds(half, half)

    def ag_copy(kind, k):
        src_blk, part_rows, to, arrival = {
            "rp": (me, lo, right, 0),
            "lm": (me, hi, left, 0),
            "rm": (me, hi, right, 1),
            "lp": (me, lo, left, 1),
            "fr": (left, lo, right, 2),
            "fl": (right, hi, left, 2),
            "po": (me, None, partner, 3),
            "pl": (left, None, partner, 3),
            "pr": (right, None, partner, 3),
            "pp": (opposite, None, partner, 3),
        }[kind]
        ref = ys.at[k, src_blk] if part_rows is None else ys.at[k, src_blk, part_rows]
        return remote(ref, ref, ag_send.at[k], ag_recv.at[arrival, k], to)

    def a1(k):
        for kind in ("rp", "lm", "rm", "lp", "po"):
            ag_copy(kind, k).start()

    def a2(k):
        settle(ys.at[k, left], ag_recv.at[0, k])
        ag_copy("fr", k).start()
        ag_copy("fl", k).start()

    def a3(k):
        settle(ys.at[k, left], ag_recv.at[1, k])
        ag_copy("pl", k).start()
        ag_copy("pr", k).start()

    def a4(k):
        settle(ys.at[k, opposite], ag_recv.at[2, k])
        ag_copy("pp", k).start()

    def a5(k):
        settle(ys.at[k, pl.ds(0, 4)], ag_recv.at[3, k])
        pltpu.make_async_copy(ys.at[k], y_out.at[k], yo_sem).start()

    def select(k):
        k2 = lax.rem(k, 2)
        r, c = iota((4 * rows, 8 * rows), 0), iota((4 * rows, 8 * rows), 1)
        sel = (c == (r // 4) * 8 + k2 * 4 + r % 4).astype(F32).astype(BF16)
        pair = xs[k // 2].reshape(8 * rows, width)
        xk[k2] = jnp.dot(sel, pair, preferred_element_type=F32).astype(BF16)

    def hidden(i):
        x = xk[lax.rem(i // blocks, 2)]
        return jax.nn.gelu(jnp.dot(x, wi_buf[lax.rem(i, W_SLOTS)], preferred_element_type=F32)).astype(BF16)

    hooks = {
        0: [(s3, 1, p) for p in range(pairs // 2 - 1, pairs)] + [(select, 1)],
        2: [(s4, 1), (select, 2)],
        3: [(a2, 0)],
        4: [(a3, 0), (select, 3)],
        5: [(a2, 1)],
        6: [(a3, 1), (a4, 0), (a2, 2)],
    }

    def ffn_step(t, carry):
        i = 2 * t
        k = i // blocks
        after = [i + 1, jnp.minimum(i + 2, steps - 1)]
        w_copies(after[0])[0].wait()
        when(i + 2 < steps, (w_copies(after[1])[0].wait,))
        w_copies(i)[1].wait()
        w_copies(i + 1)[1].wait()
        total = jnp.where(lax.rem(i, blocks) == 0, 0.0, y_acc[...])
        for n in range(2):
            h = hidden(after[n])
            total += jnp.dot(h_buf[n], wo_buf[lax.rem(i + n, W_SLOTS)], preferred_element_type=F32)
            h_buf[1 - n] = h
        y_acc[...] = total
        for n in range(2):
            when(i + n + 1 + W_SLOTS < steps, (w_copies(i + n + 1 + W_SLOTS)[0].start,))
            when(i + n + W_SLOTS < steps, (w_copies(i + n + W_SLOTS)[1].start,))

        @pl.when(lax.rem(i, blocks) == blocks - 2)
        def _():
            ys[k, me] = y_acc[...].astype(BF16)
            a1(k)

        for at, todo in hooks.items():
            when(t == at, *todo)
        return carry

    w_copies(0)[0].wait()
    select(0)
    h_buf[0] = hidden(0)
    w_copies(W_SLOTS)[0].start()
    lax.fori_loop(0, steps // 2, ffn_step, 0)
    a3(2)
    a4(1)
    a5(0)
    a4(2)
    a5(1)
    a2(3)
    a5(2)
    a3(3)
    a4(3)
    a5(3)

    def finish():
        for p in (pairs - 2, pairs - 1):
            c_copy(p).wait()
        pltpu.make_async_copy(ys, y_out, yo_sem).wait()
        settle(z_all.at[pl.ds(0, 7)], z_send)
        settle(from_partner, d_send)
        for side, relay in enumerate((relay_r, relay_l)):
            settle(relay.at[0, pl.ds(0, pairs - 1)], a_send.at[side, 0])
            settle(relay.at[1], a_send.at[side, 1])
        settle(from_opp, o_send)
        settle(from_l, b_send.at[0])
        settle(from_r, b_send.at[1])
        for k in range(4):
            settle(ys.at[k, pl.ds(0, 7)], ag_send.at[k])

    finish()


def combine_kernel(c_ref, y_ref, out_ref):
    experts, devs, eight, width = y_ref.shape
    slots = c_ref.shape[2]
    r = y_ref[...].reshape(experts * devs, eight, width).astype(F32).reshape(experts * devs * eight, width).astype(BF16)
    col, row = iota((slots, 2 * slots), 0), iota((slots, 2 * slots), 1)
    kk, core, chip, k2, s = col // 64, (col // 32) % 2, (col // 8) % 4, (col // 4) % 2, col % 4
    base = (kk * 2 + k2) * 64 + (chip * 2 + core) * 8 + s
    for which in range(2):
        spread = (row == base + which * 4).astype(F32).astype(BF16)
        c = jnp.dot(c_ref[which], spread, preferred_element_type=F32).astype(BF16)
        out_ref[which] = jnp.dot(c, r, preferred_element_type=F32).astype(BF16)


def solution(mesh):
    def shard_body(tok, lens, phi, gain, w_in, w_out):
        rows, tokens, width = tok.shape
        experts, _, ff = w_in.shape
        slots = phi.shape[1]
        pairs = rows // 2
        any_spec = pl.BlockSpec(memory_space=pl.ANY)
        smem = pl.BlockSpec(memory_space=pltpu.SMEM)
        dma = pltpu.SemaphoreType.DMA
        blk = (16, width)
        c, y = pl.pallas_call(
            route_kernel,
            out_shape=(
                jax.ShapeDtypeStruct((rows, tokens, slots), BF16),
                jax.ShapeDtypeStruct((experts, 8, 4 * rows, width), BF16),
            ),
            in_specs=[smem, smem, pl.BlockSpec(memory_space=pltpu.VMEM), any_spec, any_spec, any_spec],
            out_specs=(any_spec, any_spec),
            scratch_shapes=[
                pltpu.VMEM((TOK_SLOTS, tokens, width), BF16),
                pltpu.VMEM((width, slots), BF16),
                pltpu.VMEM((2, slots, tokens), BF16),
                pltpu.VMEM((2, slots, width), F32),
                pltpu.VMEM((2, 2, tokens, slots), BF16),
                pltpu.VMEM((2, 2, 4, pairs) + blk, BF16),
                pltpu.VMEM((2, 4, pairs) + blk, BF16),
                pltpu.VMEM((2, pairs, 16, width // 2), BF16),
                pltpu.VMEM((2, pairs, 16, width // 2), BF16),
                pltpu.VMEM((2, pairs) + blk, BF16),
                pltpu.VMEM((2, pairs) + blk, BF16),
                pltpu.VMEM(blk, BF16),
                pltpu.VMEM((2, pairs) + blk, BF16),
                pltpu.VMEM((rows, slots), F32),
                pltpu.VMEM((8, rows, slots), F32),
                pltpu.VMEM((rows, slots), F32),
                pltpu.VMEM((2, 4 * rows, width), BF16),
                pltpu.VMEM((2, 4 * rows, F_BLOCK), BF16),
                pltpu.VMEM((4 * rows, width), F32),
                pltpu.VMEM((experts, 8, 4 * rows, width), BF16),
                pltpu.VMEM((W_SLOTS, width, F_BLOCK), BF16),
                pltpu.VMEM((W_SLOTS, F_BLOCK, width), BF16),
                dma((TOK_SLOTS,)), dma((W_SLOTS,)), dma((W_SLOTS,)), dma((2,)), dma, dma, dma,
                dma, dma((2, pairs)), dma((2, 2)), dma((2, 2, pairs)), dma((2,)), dma((2, 2)), dma, dma, dma((4,)), dma((4, 4)),
            ],
            compiler_params=pltpu.CompilerParams(
                collective_id=0, has_side_effects=True, vmem_limit_bytes=67_000_000
            ),
            name="route",
        )(lens, gain, phi, tok, w_in, w_out)
        return pl.pallas_call(
            combine_kernel,
            out_shape=jax.ShapeDtypeStruct(tok.shape, BF16),
            grid=(pairs,),
            in_specs=[
                pl.BlockSpec((2, tokens, slots), lambda p: (p, 0, 0)),
                pl.BlockSpec((experts, 8, 8, width), lambda p: (0, 0, p, 0)),
            ],
            out_specs=pl.BlockSpec((2, tokens, width), lambda p: (p, 0, 0)),
            compiler_params=pltpu.CompilerParams(vmem_limit_bytes=67_000_000),
            name="combine",
        )(c, y)

    return jax.shard_map(
        shard_body,
        mesh=mesh,
        in_specs=(P("data", "seq", None), P("data"), P(None, None), P(None), P("seq", None, None), P("seq", None, None)),
        out_specs=P("data", "seq", None),
        check_vma=False,
    )
```

time: 197 us -> 85.1 us (0.43)
  Pallas kernels: 0 us -> 84.1 us
  matrix products: 81.5 us -> 0 us
  waiting for transfers between devices: 45.1 us -> 0 us
  blocking collectives: 29.2 us -> 0 us
  other arithmetic: 21.9 us -> 0 us
  between operations: 14.2 us -> 0.66 us
  local copies, waits for them, and re-layouts: 4.6 us -> 0 us
    pallas_call x0 -> x2, Pallas kernels: none -> 84.1 us  [the longest x1 69.9 us: shard_body(): pl.pallas_call(route_kernel, out_shape=(jax.ShapeDtypeStruct((rows, token...]
    dot_general x5 -> x0, matrix products: 81.5 us -> none  [the longest x1 23.8 us: shard_body(): jnp.einsum('btn,bnd->btd', combine_w, all_out, preferred_element_type=jnp...]
    all_gather x1 -> x0, waiting for transfers between devices: 28.8 us -> none  [shard_body(): all_out = lax.all_gather(slot_out, 'seq', axis=1, tiled=True)]
    reduce_scatter x1 -> x0, waiting for transfers between devices: 16.3 us -> none  [shard_body(): lax.psum_scatter(part_sum, 'seq', scatter_dimension=1, tiled=True)]
    psum x1 -> x0, blocking collectives: 15.5 us -> none  [shard_body(): col_sum = lax.psum(jnp.sum(disp_w, axis=1), 'seq')]
    reduce_sum x3 -> x0, other arithmetic: 14.7 us -> none  [the longest x1 9.86 us: shard_body(): jnp.sum(tok_f32 * tok_f32, axis=-1, keepdims=True) + 1e-06]
    pmax x1 -> x0, blocking collectives: 13.8 us -> none  [shard_body(): col_max = lax.pmax(local_max, 'seq')]
    sub x1 -> x0, other arithmetic: 5.72 us -> none  [shard_body(): combine_w = jax.nn.softmax(logits, axis=-1).astype(jnp.bfloat16)]
  transfers between devices with their start and end apart: 2 -> 0, of which waited for: 2 -> 0; matrix products, arithmetic and copies ran while one was open for 5% -> 0% of each run, Pallas kernels for 0% -> 0%
where the time goes in v2:
time: 85.1 us; the launch traced here: 84.7 us
  Pallas kernels  84.1 us (99%)
    pallas_call x1, Pallas kernels, shard_body(): pl.pallas_call(route_kernel, out_shape=(jax.ShapeDtypeStruct((rows, token...  69.9 us
    pallas_call x1, Pallas kernels, shard_body(): pl.pallas_call(combine_kernel, out_shape=jax.ShapeDtypeStruct(tok.shape,...  14.2 us

profile of v2, /device:TPU:113, one launch (start us, length us, event | category | flops | bytes accessed | tf_op | source)
XLA Modules:
  0.0 84.7 jit_solution(18238155536391957818)
XLA Ops:
  0.7 69.9 %route.1 = (bf16[16,512,128]{2,1,0:T(8,128)(2,1)}, bf16[4,8,64,1280]{3,2,1,0:T(8,128)(2,1)}) custom-call(s32[16]{0:T(128)} %lens.1, f32[1]{0:T(128)S(6)} %copy.7.gain, bf16[1280,128]{1,0:T(8,128)(2,1)} %phi.1, bf16[16,512,1280]{2,1,0:T(8,128)(2,1)} %tok.1, bf16[4,1280,5120]{2,1,0:T(8,128)(2,1)} %w_in.1, bf16[4,5120,1280]{2,1,0:T(8,128)(2,1)} %w_out.1), custom_call_target="tpu_custom_call" | custom-call | tf_op jit(solution)/shard_map/route/pallas_call | solution.py:374
  70.5 14.2 %combine.1 = bf16[16,512,1280]{2,1,0:T(8,128)(2,1)} custom-call(bf16[16,512,128]{2,1,0:T(8,128)(2,1)} %get-tuple-element.7.c_ref, bf16[4,8,64,1280]{3,2,1,0:T(8,128)(2,1)} %get-tuple-element.8.y_ref), custom_call_target="tpu_custom_call" | custom-call | tf_op jit(solution)/shard_map/combine/pallas_call | solution.py:413

commit v3 on v2

--- a/solution.py
+++ b/solution.py
@@ -11,8 +11,13 @@
 F32, BF16 = jnp.float32, jnp.bfloat16
 TOK_SLOTS = 4
 W_SLOTS = 6
+O_SLOTS = W_SLOTS + 1
+DIRECT = 1
+EARLY = 4
 F_BLOCK = 1280
 ROW_TILE = 128
+IN_SLOTS = 3
+OUT_SLOTS = 4
 
 
 def iota(shape, dim):
@@ -21,7 +26,7 @@
 
 def route_kernel(
     lens, gain, phi, tok, w_in, w_out, c_out, y_out,
-    tok_buf, phin, wt_buf, s_f32, c_buf, part, from_partner, relay_r, relay_l, from_l, from_r, from_opp, xs, z_own, z_all, z_tot,
+    phin, wt_buf, s_f32, c_buf, part, from_partner, relay_r, relay_l, from_l, from_r, from_opp, xs, z_own, z_peer, z_chip, z_all, z_tot,
     xk, h_buf, y_acc, ys, wi_buf, wo_buf,
     tok_sem, wi_sem, wo_sem, c_sem, yo_sem, z_send, z_recv,
     d_send, d_recv, a_send, a_recv, b_send, b_recv, o_send, o_recv, ag_send, ag_recv,
@@ -47,16 +52,23 @@
         peer = lax.rem(me + step, 8)
         pl.semaphore_signal(barrier, inc=1, device_id={"seq": peer}, device_id_type=MESH)
 
+    def tok_slot(b):
+        first = W_SLOTS * F_BLOCK + lax.rem(b, TOK_SLOTS) * tokens
+        return wo_buf.at[pl.ds(pl.multiple_of(first, 256), tokens)]
+
+    def wo_slot(i):
+        return wo_buf.at[pl.ds(pl.multiple_of(lax.rem(i, O_SLOTS) * F_BLOCK, 256), F_BLOCK)]
+
     def tok_copy(b):
-        slot = lax.rem(b, TOK_SLOTS)
-        return pltpu.make_async_copy(tok.at[b], tok_buf.at[slot], tok_sem.at[slot])
+        return pltpu.make_async_copy(tok.at[b], tok_slot(b), tok_sem.at[lax.rem(b, TOK_SLOTS)])
 
     def w_copies(i):
-        e, f, slot = i // blocks, lax.rem(i, blocks), lax.rem(i, W_SLOTS)
+        e, f = i // blocks, lax.rem(i, blocks)
         cols = pl.ds(pl.multiple_of(f * F_BLOCK, F_BLOCK), F_BLOCK)
+        i_slot = lax.rem(i, W_SLOTS)
         return (
-            pltpu.make_async_copy(w_in.at[e, :, cols], wi_buf.at[slot], wi_sem.at[slot]),
-            pltpu.make_async_copy(w_out.at[e, cols, :], wo_buf.at[slot], wo_sem.at[slot]),
+            pltpu.make_async_copy(w_in.at[e, :, cols], wi_buf.at[i_slot], wi_sem.at[i_slot]),
+            pltpu.make_async_copy(w_out.at[e, cols, :], wo_slot(i), wo_sem.at[lax.rem(i, O_SLOTS)]),
         )
 
     for b in range(TOK_SLOTS):
@@ -84,7 +96,7 @@
     def one_pair(p):
         for which in range(2):
             b = 2 * p + which
-            x_ref = tok_buf.at[lax.rem(b, TOK_SLOTS)]
+            x_ref = tok_slot(b)
             length = lens[b]
             z_row = jnp.zeros((1, slots), F32)
             for r in range(tokens // ROW_TILE):
@@ -139,19 +151,13 @@
         for kind in ("ap", "am", "bp0", "bm0"):
             rs_copy(kind, kk, p).start()
 
-    def last_copies():
-        p = pairs - 1
+    def s2_direct(p):
+        chip_sum(0, p)
         mine = part.at[0, core]
-        return (
-            remote(mine.at[c_opp, p], from_opp, o_send, o_recv, opposite),
-            remote(mine.at[c_right, p], from_l.at[0, p], b_send.at[0], b_recv.at[0, 0], right),
-            remote(mine.at[c_left, p], from_r.at[0, p], b_send.at[1], b_recv.at[1, 0], left),
-        )
-
-    def s2_last():
-        chip_sum(0, pairs - 1)
-        for copy in last_copies():
-            copy.start()
+        n = p - (pairs - DIRECT)
+        remote(mine.at[c_opp, p], from_opp.at[n], o_send, o_recv, opposite).start()
+        remote(mine.at[c_right, p], from_l.at[0, p], b_send.at[0], b_recv.at[0, 0], right).start()
+        remote(mine.at[c_left, p], from_r.at[0, p], b_send.at[1], b_recv.at[1, 0], left).start()
 
     def s3(kk, p):
         for kind, then, c, relay, cols in (
@@ -176,13 +182,15 @@
             settle(from_opp, o_recv)
         for p in range(pairs):
             total = part[kk, core, chip, p].astype(F32) + from_l[kk, p].astype(F32) + from_r[kk, p].astype(F32)
-            if kk == 0 and p == pairs - 1:
-                total += from_opp[...].astype(F32)
+            if kk == 0 and p >= pairs - DIRECT:
+                total += from_opp[p - (pairs - DIRECT)].astype(F32)
             xs[kk, p] = (total / cols[p]).astype(BF16)
 
-    def z_copy(step):
-        peer = lax.rem(me + step, 8)
-        return remote(z_own, z_all.at[me], z_send, z_recv, peer)
+    def z_pair():
+        return remote(z_own, z_peer, z_send.at[0], z_recv.at[0], partner)
+
+    def z_chips():
+        return [remote(z_chip, z_all.at[chip], z_send.at[1], z_recv.at[1], to) for to in (right, left, opposite)]
 
     def when(condition, *todo):
         @pl.when(condition)
@@ -195,41 +203,57 @@
         for which in range(2):
             tok_copy(2 * p + which).wait()
         one_pair(p)
+        when(p == pairs - 1, (lambda: z_pair().start(),))
         d2d(0, p).start()
         d2d(1, p).start()
         c_copy(p).start()
         for which in range(2):
             b = 2 * p + TOK_SLOTS + which
             when(b < rows, (lambda b=b: tok_copy(b).start(),))
-        when(p < W_SLOTS, (lambda: [copy.start() for copy in w_copies(p)],))
-        odd = lax.rem(p, 2)
-        when(p >= 1, (s2, 0, p - 1))
+        for n in range(2 * W_SLOTS):
+            when(p == n * pairs // (2 * W_SLOTS), (w_copies(n // 2)[n % 2].start,))
+        when((p >= 1) & (p <= pairs - DIRECT), (s2, 0, p - 1))
+        when(p > pairs - DIRECT, (s2_direct, p - 1))
         when(p >= 3, (s3, 0, p - 3))
-        when((p >= 4) & (odd == 0), (s3, 1, p // 2 - 2))
-        when((p >= 2) & (odd == 0), (s2, 1, p // 2 - 1))
+        when((p >= 1) & (p <= EARLY), (s2, 1, p - 1))
+        when(p >= pairs - EARLY, (s3, 1, p - (pairs - EARLY)))
         return carry
 
     pl.semaphore_wait(barrier, 7)
     lax.fori_loop(0, pairs, pair_step, 0)
-    for step in range(1, 8):
-        z_copy(step).start()
-    s2_last()
-    s3(0, pairs - 3)
-    s3(0, pairs - 2)
-    s3(1, pairs // 2 - 2)
-    for p in range(pairs // 2 - 1, pairs):
+    w_copies(W_SLOTS)[1].start()
+    s2_direct(pairs - 1)
+    z_pair().wait_recv()
+    z_chip[...] = z_own[...] + z_peer[...]
+    for copy in z_chips():
+        copy.start()
+    for p in range(pairs - 3, pairs - DIRECT):
+        s3(0, p)
+    for p in range(EARLY, pairs):
         s2(1, p)
-    settle(z_all.at[pl.ds(0, 7)], z_recv)
-    z = z_own[...]
-    for step in range(1, 8):
-        z += z_all[lax.rem(me + step, 8)]
+    settle(z_all.at[pl.ds(0, 3)], z_recv.at[1])
+    z = z_chip[...]
+    for c in (c_right, c_left, c_opp):
+        z += z_all[c]
     z_tot[...] = z
     s4(0)
 
     half = 2 * rows
     lo, hi = pl.ds(0, half), pl.ds(half, half)
 
-    def ag_copy(kind, k):
+    split = 3 * (width // 5)
+    pieces = 2 + experts - 1
+
+    def piece(c):
+        if isinstance(c, int) and c >= experts - 1:
+            return experts - 1, pl.ds(0, split) if c == experts - 1 else pl.ds(split, width - split)
+        return c, pl.ds(0, width)
+
+    def blk_of(c, d, part_rows=pl.ds(0, 4 * rows)):
+        k, cols = piece(c)
+        return ys.at[k, d, part_rows, cols]
+
+    def ag_copy(kind, c):
         src_blk, part_rows, to, arrival = {
             "rp": (me, lo, right, 0),
             "lm": (me, hi, left, 0),
@@ -242,30 +266,31 @@
             "pr": (right, None, partner, 3),
             "pp": (opposite, None, partner, 3),
         }[kind]
-        ref = ys.at[k, src_blk] if part_rows is None else ys.at[k, src_blk, part_rows]
-        return remote(ref, ref, ag_send.at[k], ag_recv.at[arrival, k], to)
-
-    def a1(k):
+        ref = blk_of(c, src_blk) if part_rows is None else blk_of(c, src_blk, part_rows)
+        return remote(ref, ref, ag_send.at[c], ag_recv.at[arrival, c], to)
+
+    def a1(c):
         for kind in ("rp", "lm", "rm", "lp", "po"):
-            ag_copy(kind, k).start()
-
-    def a2(k):
-        settle(ys.at[k, left], ag_recv.at[0, k])
-        ag_copy("fr", k).start()
-        ag_copy("fl", k).start()
-
-    def a3(k):
-        settle(ys.at[k, left], ag_recv.at[1, k])
-        ag_copy("pl", k).start()
-        ag_copy("pr", k).start()
-
-    def a4(k):
-        settle(ys.at[k, opposite], ag_recv.at[2, k])
-        ag_copy("pp", k).start()
-
-    def a5(k):
-        settle(ys.at[k, pl.ds(0, 4)], ag_recv.at[3, k])
-        pltpu.make_async_copy(ys.at[k], y_out.at[k], yo_sem).start()
+            ag_copy(kind, c).start()
+
+    def a2(c):
+        settle(blk_of(c, left), ag_recv.at[0, c])
+        ag_copy("fr", c).start()
+        ag_copy("fl", c).start()
+
+    def a3(c):
+        settle(blk_of(c, left), ag_recv.at[1, c])
+        ag_copy("pl", c).start()
+        ag_copy("pr", c).start()
+
+    def a4(c):
+        settle(blk_of(c, opposite), ag_recv.at[2, c])
+        ag_copy("pp", c).start()
+
+    def a5(c):
+        settle(blk_of(c, pl.ds(0, 4)), ag_recv.at[3, c])
+        k, cols = piece(c)
+        pltpu.make_async_copy(ys.at[k, :, :, cols], y_out.at[k, :, :, cols], yo_sem).start()
 
     def select(k):
         k2 = lax.rem(k, 2)
@@ -279,31 +304,35 @@
         return jax.nn.gelu(jnp.dot(x, wi_buf[lax.rem(i, W_SLOTS)], preferred_element_type=F32)).astype(BF16)
 
     hooks = {
-        0: [(s3, 1, p) for p in range(pairs // 2 - 1, pairs)] + [(select, 1)],
+        0: [(s3, 1, p) for p in range(EARLY, pairs)] + [(select, 1)],
         2: [(s4, 1), (select, 2)],
         3: [(a2, 0)],
         4: [(a3, 0), (select, 3)],
         5: [(a2, 1)],
-        6: [(a3, 1), (a4, 0), (a2, 2)],
+        6: [(a3, 1), (a4, 0)],
     }
+
+    def wo(i):
+        return wo_slot(i)[...]
+
+    def refill(i):
+        when(i + 1 + W_SLOTS < steps, (lambda: w_copies(i + 1 + W_SLOTS)[0].start(),))
+        when(i + O_SLOTS < steps, (lambda: w_copies(i + O_SLOTS)[1].start(),))
 
     def ffn_step(t, carry):
         i = 2 * t
         k = i // blocks
-        after = [i + 1, jnp.minimum(i + 2, steps - 1)]
-        w_copies(after[0])[0].wait()
-        when(i + 2 < steps, (w_copies(after[1])[0].wait,))
-        w_copies(i)[1].wait()
-        w_copies(i + 1)[1].wait()
+        for n in range(2):
+            w_copies(i + n + 1)[0].wait()
+            w_copies(i + n)[1].wait()
         total = jnp.where(lax.rem(i, blocks) == 0, 0.0, y_acc[...])
         for n in range(2):
-            h = hidden(after[n])
-            total += jnp.dot(h_buf[n], wo_buf[lax.rem(i + n, W_SLOTS)], preferred_element_type=F32)
+            h = hidden(i + n + 1)
+            total += jnp.dot(h_buf[n], wo(i + n), preferred_element_type=F32)
             h_buf[1 - n] = h
         y_acc[...] = total
         for n in range(2):
-            when(i + n + 1 + W_SLOTS < steps, (w_copies(i + n + 1 + W_SLOTS)[0].start,))
-            when(i + n + W_SLOTS < steps, (w_copies(i + n + W_SLOTS)[1].start,))
+            refill(i + n)
 
         @pl.when(lax.rem(i, blocks) == blocks - 2)
         def _():
@@ -318,7 +347,20 @@
     select(0)
     h_buf[0] = hidden(0)
     w_copies(W_SLOTS)[0].start()
-    lax.fori_loop(0, steps // 2, ffn_step, 0)
+    lax.fori_loop(0, steps // 2 - 1, ffn_step, 0)
+
+    w_copies(steps - 1)[0].wait()
+    h_buf[1] = hidden(steps - 1)
+    a2(2)
+    for n in range(2):
+        w_copies(steps - 2 + n)[1].wait()
+    for c in (experts - 1, experts):
+        cols = piece(c)[1]
+        total = y_acc[:, cols]
+        for n in range(2):
+            total += jnp.dot(h_buf[n], wo_slot(steps - 2 + n)[:, cols], preferred_element_type=F32)
+        ys[experts - 1, me, :, cols] = total.astype(BF16)
+        a1(c)
     a3(2)
     a4(1)
     a5(0)
@@ -327,38 +369,89 @@
     a2(3)
     a5(2)
     a3(3)
+    a2(4)
+    a3(4)
     a4(3)
+    a4(4)
     a5(3)
+    a5(4)
 
     def finish():
         for p in (pairs - 2, pairs - 1):
             c_copy(p).wait()
         pltpu.make_async_copy(ys, y_out, yo_sem).wait()
-        settle(z_all.at[pl.ds(0, 7)], z_send)
+        settle(z_peer, z_send.at[0])
+        settle(z_all.at[pl.ds(0, 3)], z_send.at[1])
         settle(from_partner, d_send)
         for side, relay in enumerate((relay_r, relay_l)):
-            settle(relay.at[0, pl.ds(0, pairs - 1)], a_send.at[side, 0])
+            settle(relay.at[0, pl.ds(0, pairs - DIRECT)], a_send.at[side, 0])
             settle(relay.at[1], a_send.at[side, 1])
         settle(from_opp, o_send)
         settle(from_l, b_send.at[0])
         settle(from_r, b_send.at[1])
-        for k in range(4):
-            settle(ys.at[k, pl.ds(0, 7)], ag_send.at[k])
+        for c in range(pieces):
+            settle(blk_of(c, pl.ds(0, 7)), ag_send.at[c])
 
     finish()
 
 
-def combine_kernel(c_ref, y_ref, out_ref):
-    experts, devs, eight, width = y_ref.shape
-    slots = c_ref.shape[2]
-    r = y_ref[...].reshape(experts * devs, eight, width).astype(F32).reshape(experts * devs * eight, width).astype(BF16)
-    col, row = iota((slots, 2 * slots), 0), iota((slots, 2 * slots), 1)
-    kk, core, chip, k2, s = col // 64, (col // 32) % 2, (col // 8) % 4, (col // 4) % 2, col % 4
-    base = (kk * 2 + k2) * 64 + (chip * 2 + core) * 8 + s
-    for which in range(2):
-        spread = (row == base + which * 4).astype(F32).astype(BF16)
-        c = jnp.dot(c_ref[which], spread, preferred_element_type=F32).astype(BF16)
-        out_ref[which] = jnp.dot(c, r, preferred_element_type=F32).astype(BF16)
+def combine_kernel(c_hbm, y_hbm, out_hbm, c_buf, y_buf, out_buf, c_sem, y_sem, out_sem):
+    rows = out_hbm.shape[0]
+    width = out_hbm.shape[2]
+    low = iota((8, width), 0) < 4
+
+    def loads(p):
+        slot = lax.rem(p, IN_SLOTS)
+        eight = pl.ds(pl.multiple_of(8 * p, 8), 8)
+        return (
+            pltpu.make_async_copy(y_hbm.at[:, :, eight], y_buf.at[slot], y_sem.at[slot]),
+            pltpu.make_async_copy(c_hbm.at[pl.ds(2 * p, 2)], c_buf.at[slot], c_sem.at[slot]),
+        )
+
+    def store(b):
+        slot = lax.rem(b, OUT_SLOTS)
+        return pltpu.make_async_copy(out_buf.at[slot], out_hbm.at[b], out_sem.at[slot])
+
+    def slot_rows(y_ref):
+        first, second = [], []
+        for kk in range(2):
+            for core in range(2):
+                for chip in range(4):
+                    even = y_ref[2 * kk, chip * 2 + core].astype(F32)
+                    odd = y_ref[2 * kk + 1, chip * 2 + core].astype(F32)
+                    first.append(jnp.where(low, even, pltpu.roll(odd, 4, 0)))
+                    second.append(jnp.where(low, pltpu.roll(even, 4, 0), odd))
+        return [jnp.concatenate(tiles, axis=0).astype(BF16) for tiles in (first, second)]
+
+    def step(p, carry):
+        for copy in loads(p):
+            copy.wait()
+        slot = lax.rem(p, IN_SLOTS)
+        y = slot_rows(y_buf.at[slot])
+        for which in range(2):
+            b = 2 * p + which
+
+            @pl.when(b >= OUT_SLOTS)
+            def _():
+                store(b - OUT_SLOTS).wait()
+
+            mixed = jnp.dot(c_buf[slot, which], y[which], preferred_element_type=F32)
+            out_buf[lax.rem(b, OUT_SLOTS)] = mixed.astype(BF16)
+            store(b).start()
+
+        @pl.when(p + IN_SLOTS < rows // 2)
+        def _():
+            for copy in loads(p + IN_SLOTS):
+                copy.start()
+
+        return carry
+
+    for p in range(IN_SLOTS):
+        for copy in loads(p):
+            copy.start()
+    lax.fori_loop(0, rows // 2, step, 0)
+    for b in range(rows - OUT_SLOTS, rows):
+        store(b).wait()
 
 
 def solution(mesh):
@@ -380,7 +473,6 @@
             in_specs=[smem, smem, pl.BlockSpec(memory_space=pltpu.VMEM), any_spec, any_spec, any_spec],
             out_specs=(any_spec, any_spec),
             scratch_shapes=[
-                pltpu.VMEM((TOK_SLOTS, tokens, width), BF16),
                 pltpu.VMEM((width, slots), BF16),
                 pltpu.VMEM((2, slots, tokens), BF16),
                 pltpu.VMEM((2, slots, width), F32),
@@ -391,19 +483,21 @@
                 pltpu.VMEM((2, pairs, 16, width // 2), BF16),
                 pltpu.VMEM((2, pairs) + blk, BF16),
                 pltpu.VMEM((2, pairs) + blk, BF16),
-                pltpu.VMEM(blk, BF16),
+                pltpu.VMEM((DIRECT,) + blk, BF16),
                 pltpu.VMEM((2, pairs) + blk, BF16),
                 pltpu.VMEM((rows, slots), F32),
-                pltpu.VMEM((8, rows, slots), F32),
+                pltpu.VMEM((rows, slots), F32),
+                pltpu.VMEM((rows, slots), F32),
+                pltpu.VMEM((4, rows, slots), F32),
                 pltpu.VMEM((rows, slots), F32),
                 pltpu.VMEM((2, 4 * rows, width), BF16),
                 pltpu.VMEM((2, 4 * rows, F_BLOCK), BF16),
                 pltpu.VMEM((4 * rows, width), F32),
                 pltpu.VMEM((experts, 8, 4 * rows, width), BF16),
                 pltpu.VMEM((W_SLOTS, width, F_BLOCK), BF16),
-                pltpu.VMEM((W_SLOTS, F_BLOCK, width), BF16),
-                dma((TOK_SLOTS,)), dma((W_SLOTS,)), dma((W_SLOTS,)), dma((2,)), dma, dma, dma,
-                dma, dma((2, pairs)), dma((2, 2)), dma((2, 2, pairs)), dma((2,)), dma((2, 2)), dma, dma, dma((4,)), dma((4, 4)),
+                pltpu.VMEM((W_SLOTS * F_BLOCK + max(F_BLOCK, TOK_SLOTS * tokens), width), BF16),
+                dma((TOK_SLOTS,)), dma((W_SLOTS,)), dma((O_SLOTS,)), dma((2,)), dma, dma((2,)), dma((2,)),
+                dma, dma((2, pairs)), dma((2, 2)), dma((2, 2, pairs)), dma((2,)), dma((2, 2)), dma, dma, dma((experts + 1,)), dma((4, experts + 1)),
             ],
             compiler_params=pltpu.CompilerParams(
                 collective_id=0, has_side_effects=True, vmem_limit_bytes=67_000_000
@@ -413,12 +507,14 @@
         return pl.pallas_call(
             combine_kernel,
             out_shape=jax.ShapeDtypeStruct(tok.shape, BF16),
-            grid=(pairs,),
-            in_specs=[
-                pl.BlockSpec((2, tokens, slots), lambda p: (p, 0, 0)),
-                pl.BlockSpec((experts, 8, 8, width), lambda p: (0, 0, p, 0)),
+            in_specs=[any_spec, any_spec],
+            out_specs=any_spec,
+            scratch_shapes=[
+                pltpu.VMEM((IN_SLOTS, 2, tokens, slots), BF16),
+                pltpu.VMEM((IN_SLOTS, experts, 8, 8, width), BF16),
+                pltpu.VMEM((OUT_SLOTS, tokens, width), BF16),
+                dma((IN_SLOTS,)), dma((IN_SLOTS,)), dma((OUT_SLOTS,)),
             ],
-            out_specs=pl.BlockSpec((2, tokens, width), lambda p: (p, 0, 0)),
             compiler_params=pltpu.CompilerParams(vmem_limit_bytes=67_000_000),
             name="combine",
         )(c, y)

time: 85.1 us -> 81 us (0.952)
  Pallas kernels: 84.1 us -> 80.2 us
    pallas_call x1, Pallas kernels: 69.9 us -> 67.8 us  [shard_body(): pl.pallas_call(route_kernel, out_shape=(jax.ShapeDtypeStruct((rows, token...]
    pallas_call x1, Pallas kernels: 14.2 us -> 12.4 us  [shard_body(): pl.pallas_call(combine_kernel, out_shape=jax.ShapeDtypeStruct(tok.shape,...]
where the time goes in v3:
time: 81 us; the launch traced here: 80.8 us
  Pallas kernels  80.2 us (99%)
    pallas_call x1, Pallas kernels, shard_body(): pl.pallas_call(route_kernel, out_shape=(jax.ShapeDtypeStruct((rows, token...  67.8 us
    pallas_call x1, Pallas kernels, shard_body(): pl.pallas_call(combine_kernel, out_shape=jax.ShapeDtypeStruct(tok.shape,...  12.4 us

profile of v3, /device:TPU:113, one launch (start us, length us, event | category | flops | bytes accessed | tf_op | source)
XLA Modules:
  0.0 80.8 jit_solution(6843289402970526145)
XLA Ops:
  0.7 67.8 %route.1 = (bf16[16,512,128]{2,1,0:T(8,128)(2,1)}, bf16[4,8,64,1280]{3,2,1,0:T(8,128)(2,1)}) custom-call(s32[16]{0:T(128)} %lens.1, f32[1]{0:T(128)S(6)} %copy.7.gain, bf16[1280,128]{1,0:T(8,128)(2,1)} %phi.1, bf16[16,512,1280]{2,1,0:T(8,128)(2,1)} %tok.1, bf16[4,1280,5120]{2,1,0:T(8,128)(2,1)} %w_in.1, bf16[4,5120,1280]{2,1,0:T(8,128)(2,1)} %w_out.1), custom_call_target="tpu_custom_call" | custom-call | tf_op jit(solution)/shard_map/route/pallas_call | solution.py:467
  68.5 12.4 %combine.1 = bf16[16,512,1280]{2,1,0:T(8,128)(2,1)} custom-call(bf16[16,512,128]{2,1,0:T(8,128)(2,1)} %get-tuple-element.7.c_hbm, bf16[4,8,64,1280]{3,2,1,0:T(8,128)(2,1)} %get-tuple-element.8.y_hbm), custom_call_target="tpu_custom_call" | custom-call | tf_op jit(solution)/shard_map/combine/pallas_call | solution.py:507

commit v4 on v3

--- a/solution.py
+++ b/solution.py
@@ -12,7 +12,6 @@
 TOK_SLOTS = 4
 W_SLOTS = 6
 O_SLOTS = W_SLOTS + 1
-DIRECT = 1
 EARLY = 4
 F_BLOCK = 1280
 ROW_TILE = 128
@@ -26,9 +25,9 @@
 
 def route_kernel(
     lens, gain, phi, tok, w_in, w_out, c_out, y_out,
-    phin, wt_buf, s_f32, c_buf, part, from_partner, relay_r, relay_l, from_l, from_r, from_opp, xs, z_own, z_peer, z_chip, z_all, z_tot,
-    xk, h_buf, y_acc, ys, wi_buf, wo_buf,
-    tok_sem, wi_sem, wo_sem, c_sem, yo_sem, z_send, z_recv,
+    phin, wt_buf, s_f32, c_buf, part, from_partner, relay, from_l, from_r, xs, z_own, z_peer, z_chip, z_all, z_tot,
+    xk, h_buf, ys, wi_buf, wo_buf,
+    phi_sem, tok_sem, wi_sem, wo_sem, c_sem, yo_sem, z_send, z_recv,
     d_send, d_recv, a_send, a_recv, b_send, b_recv, o_send, o_recv, ag_send, ag_recv,
 ):
     rows, tokens, width = tok.shape
@@ -71,11 +70,14 @@
             pltpu.make_async_copy(w_out.at[e, cols, :], wo_slot(i), wo_sem.at[lax.rem(i, O_SLOTS)]),
         )
 
-    for b in range(TOK_SLOTS):
-        tok_copy(b).start()
+    phi_copy = pltpu.make_async_copy(phi, phin, phi_sem)
+    tok_copy(0).start()
+    phi_copy.start()
+    tok_copy(1).start()
 
     gain_s = gain[0]
-    phi_f32 = phi[...].astype(F32)
+    phi_copy.wait()
+    phi_f32 = phin[...].astype(F32)
     col_inv = lax.rsqrt(jnp.sum(phi_f32 * phi_f32, axis=0, keepdims=True) + 1e-6)
     phi_n = (phi_f32 * (gain_s * col_inv)).astype(BF16)
     src, dst = iota((slots, slots), 0), iota((slots, slots), 1)
@@ -83,6 +85,9 @@
     perm = (src == cc * 32 + hh * 16 + kk * 8 + rest).astype(F32).astype(BF16)
     phin[...] = jnp.dot(phi_n, perm, preferred_element_type=F32).astype(BF16)
 
+    for b in range(2, TOK_SLOTS):
+        tok_copy(b).start()
+
     def c_copy(p):
         slot = lax.rem(p, 2)
         return pltpu.make_async_copy(c_buf.at[slot], c_out.at[pl.ds(2 * p, 2)], c_sem.at[slot])
@@ -93,28 +98,26 @@
             both = jnp.concatenate([s_f32[0, eight, :], s_f32[1, eight, :]], axis=0)
             part[g // 8, (g // 4) % 2, g % 4, p] = both.astype(BF16)
 
-    def one_pair(p):
-        for which in range(2):
-            b = 2 * p + which
-            x_ref = tok_slot(b)
-            length = lens[b]
-            z_row = jnp.zeros((1, slots), F32)
-            for r in range(tokens // ROW_TILE):
-                tile = pl.ds(r * ROW_TILE, ROW_TILE)
-                x = x_ref[tile, :].astype(F32)
-                inv = lax.rsqrt(jnp.sum(x * x, axis=-1, keepdims=True) + 1e-6)
-                logits = jnp.dot((x * inv).astype(BF16), phin[...], preferred_element_type=F32)
-                e = jnp.exp(logits - gain_s)
-                pos = me * tokens + r * ROW_TILE + iota((ROW_TILE, slots), 0)
-                valid = pos < length
-                total = jnp.sum(e, axis=-1, keepdims=True)
-                c_buf[lax.rem(p, 2), which, tile, :] = jnp.where(valid, e / total, 0.0).astype(BF16)
-                w = jnp.where(valid, e, 0.0)
-                z_row += jnp.sum(w, axis=0, keepdims=True)
-                wt_buf[which, :, tile] = w.T.astype(BF16)
-            z_own[pl.ds(b, 1), :] = z_row
-            s_f32[which] = jnp.dot(wt_buf[which], x_ref[...], preferred_element_type=F32)
-        pack_pair(p)
+    def one_row(p, which):
+        b = 2 * p + which
+        x_ref = tok_slot(b)
+        length = lens[b]
+        z_row = jnp.zeros((1, slots), F32)
+        for r in range(tokens // ROW_TILE):
+            tile = pl.ds(r * ROW_TILE, ROW_TILE)
+            x = x_ref[tile, :].astype(F32)
+            inv = lax.rsqrt(jnp.sum(x * x, axis=-1, keepdims=True) + 1e-6)
+            logits = jnp.dot((x * inv).astype(BF16), phin[...], preferred_element_type=F32)
+            e = jnp.exp(logits - gain_s)
+            pos = me * tokens + r * ROW_TILE + iota((ROW_TILE, slots), 0)
+            valid = pos < length
+            total = jnp.sum(e, axis=-1, keepdims=True)
+            c_buf[lax.rem(p, 2), which, tile, :] = jnp.where(valid, e / total, 0.0).astype(BF16)
+            w = jnp.where(valid, e, 0.0)
+            z_row += jnp.sum(w, axis=0, keepdims=True)
+            wt_buf[which, :, tile] = w.T.astype(BF16)
+        z_own[pl.ds(b, 1), :] = z_row
+        s_f32[which] = jnp.dot(wt_buf[which], x_ref[...], preferred_element_type=F32)
 
     def remote(src_ref, dst_ref, send, recv, to):
         return pltpu.make_async_remote_copy(
@@ -134,8 +137,8 @@
         to_right = kind[1] == "p"
         side, to = (0, right) if to_right else (1, left)
         if kind[0] == "a":
-            cols, relay = (lo_cols, relay_r) if to_right else (hi_cols, relay_l)
-            return remote(mine.at[c_opp, p, :, cols], relay.at[kk, p], a_send.at[side, kk], a_recv.at[side, kk, p], to)
+            cols = lo_cols if to_right else hi_cols
+            return remote(mine.at[c_opp, p, :, cols], relay.at[kk, p, :, cols], a_send.at[side, kk], a_recv.at[side, kk, p], to)
         cols = hi_cols if kind in ("bp0", "bm1") else lo_cols
         c, inbox = (c_right, from_l) if to_right else (c_left, from_r)
         return remote(mine.at[c, p, :, cols], inbox.at[kk, p, :, cols], b_send.at[side], b_recv.at[side, kk], to)
@@ -154,18 +157,14 @@
     def s2_direct(p):
         chip_sum(0, p)
         mine = part.at[0, core]
-        n = p - (pairs - DIRECT)
-        remote(mine.at[c_opp, p], from_opp.at[n], o_send, o_recv, opposite).start()
+        remote(mine.at[c_opp, p], relay.at[0, p], o_send, o_recv, opposite).start()
         remote(mine.at[c_right, p], from_l.at[0, p], b_send.at[0], b_recv.at[0, 0], right).start()
         remote(mine.at[c_left, p], from_r.at[0, p], b_send.at[1], b_recv.at[1, 0], left).start()
 
     def s3(kk, p):
-        for kind, then, c, relay, cols in (
-            ("ap", "bp1", c_right, relay_r, lo_cols),
-            ("am", "bm1", c_left, relay_l, hi_cols),
-        ):
+        for kind, then, c, cols in (("ap", "bp1", c_right, lo_cols), ("am", "bm1", c_left, hi_cols)):
             rs_copy(kind, kk, p).wait_recv()
-            total = part[kk, core, c, p, :, cols].astype(F32) + relay[kk, p].astype(F32)
+            total = part[kk, core, c, p, :, cols].astype(F32) + relay[kk, p, :, cols].astype(F32)
             part[kk, core, c, p, :, cols] = total.astype(BF16)
             rs_copy(then, kk, p).start()
 
@@ -179,11 +178,11 @@
         settle(from_l.at[kk], b_recv.at[0, kk])
         settle(from_r.at[kk], b_recv.at[1, kk])
         if kk == 0:
-            settle(from_opp, o_recv)
+            settle(relay.at[0, pairs - 1], o_recv)
         for p in range(pairs):
             total = part[kk, core, chip, p].astype(F32) + from_l[kk, p].astype(F32) + from_r[kk, p].astype(F32)
-            if kk == 0 and p >= pairs - DIRECT:
-                total += from_opp[p - (pairs - DIRECT)].astype(F32)
+            if kk == 0 and p == pairs - 1:
+                total += relay[0, p].astype(F32)
             xs[kk, p] = (total / cols[p]).astype(BF16)
 
     def z_pair():
@@ -202,7 +201,9 @@
         when(p >= 2, (lambda: c_copy(p - 2).wait(),))
         for which in range(2):
             tok_copy(2 * p + which).wait()
-        one_pair(p)
+        for which in range(2):
+            one_row(p, which)
+        pack_pair(p)
         when(p == pairs - 1, (lambda: z_pair().start(),))
         d2d(0, p).start()
         d2d(1, p).start()
@@ -212,8 +213,7 @@
             when(b < rows, (lambda b=b: tok_copy(b).start(),))
         for n in range(2 * W_SLOTS):
             when(p == n * pairs // (2 * W_SLOTS), (w_copies(n // 2)[n % 2].start,))
-        when((p >= 1) & (p <= pairs - DIRECT), (s2, 0, p - 1))
-        when(p > pairs - DIRECT, (s2_direct, p - 1))
+        when(p >= 1, (s2, 0, p - 1))
         when(p >= 3, (s3, 0, p - 3))
         when((p >= 1) & (p <= EARLY), (s2, 1, p - 1))
         when(p >= pairs - EARLY, (s3, 1, p - (pairs - EARLY)))
@@ -222,13 +222,13 @@
     pl.semaphore_wait(barrier, 7)
     lax.fori_loop(0, pairs, pair_step, 0)
     w_copies(W_SLOTS)[1].start()
-    s2_direct(pairs - 1)
     z_pair().wait_recv()
     z_chip[...] = z_own[...] + z_peer[...]
     for copy in z_chips():
         copy.start()
-    for p in range(pairs - 3, pairs - DIRECT):
-        s3(0, p)
+    s2_direct(pairs - 1)
+    s3(0, pairs - 3)
+    s3(0, pairs - 2)
     for p in range(EARLY, pairs):
         s2(1, p)
     settle(z_all.at[pl.ds(0, 3)], z_recv.at[1])
@@ -292,6 +292,8 @@
         k, cols = piece(c)
         pltpu.make_async_copy(ys.at[k, :, :, cols], y_out.at[k, :, :, cols], yo_sem).start()
 
+    y_acc = s_f32.at[0, pl.ds(0, 4 * rows)]
+
     def select(k):
         k2 = lax.rem(k, 2)
         r, c = iota((4 * rows, 8 * rows), 0), iota((4 * rows, 8 * rows), 1)
@@ -315,11 +317,7 @@
     def wo(i):
         return wo_slot(i)[...]
 
-    def refill(i):
-        when(i + 1 + W_SLOTS < steps, (lambda: w_copies(i + 1 + W_SLOTS)[0].start(),))
-        when(i + O_SLOTS < steps, (lambda: w_copies(i + O_SLOTS)[1].start(),))
-
-    def ffn_step(t, carry):
+    def ffn_step(early, t, carry):
         i = 2 * t
         k = i // blocks
         for n in range(2):
@@ -330,9 +328,13 @@
             h = hidden(i + n + 1)
             total += jnp.dot(h_buf[n], wo(i + n), preferred_element_type=F32)
             h_buf[1 - n] = h
+            if early and n == 0:
+                w_copies(i + 1 + W_SLOTS)[0].start()
+                w_copies(i + O_SLOTS)[1].start()
         y_acc[...] = total
-        for n in range(2):
-            refill(i + n)
+        if early:
+            when(i + 2 + W_SLOTS < steps, (lambda: w_copies(i + 2 + W_SLOTS)[0].start(),))
+            when(i + 1 + O_SLOTS < steps, (lambda: w_copies(i + 1 + O_SLOTS)[1].start(),))
 
         @pl.when(lax.rem(i, blocks) == blocks - 2)
         def _():
@@ -347,7 +349,9 @@
     select(0)
     h_buf[0] = hidden(0)
     w_copies(W_SLOTS)[0].start()
-    lax.fori_loop(0, steps // 2 - 1, ffn_step, 0)
+    fetching = (steps - O_SLOTS + 1) // 2
+    lax.fori_loop(0, fetching, functools.partial(ffn_step, True), 0)
+    lax.fori_loop(fetching, steps // 2 - 1, functools.partial(ffn_step, False), 0)
 
     w_copies(steps - 1)[0].wait()
     h_buf[1] = hidden(steps - 1)
@@ -383,10 +387,10 @@
         settle(z_peer, z_send.at[0])
         settle(z_all.at[pl.ds(0, 3)], z_send.at[1])
         settle(from_partner, d_send)
-        for side, relay in enumerate((relay_r, relay_l)):
-            settle(relay.at[0, pl.ds(0, pairs - DIRECT)], a_send.at[side, 0])
-            settle(relay.at[1], a_send.at[side, 1])
-        settle(from_opp, o_send)
+        for side, cols in enumerate((lo_cols, hi_cols)):
+            settle(relay.at[0, pl.ds(0, pairs - 1), :, cols], a_send.at[side, 0])
+            settle(relay.at[1, :, :, cols], a_send.at[side, 1])
+        settle(relay.at[0, pairs - 1], o_send)
         settle(from_l, b_send.at[0])
         settle(from_r, b_send.at[1])
         for c in range(pieces):
@@ -470,7 +474,7 @@
                 jax.ShapeDtypeStruct((rows, tokens, slots), BF16),
                 jax.ShapeDtypeStruct((experts, 8, 4 * rows, width), BF16),
             ),
-            in_specs=[smem, smem, pl.BlockSpec(memory_space=pltpu.VMEM), any_spec, any_spec, any_spec],
+            in_specs=[smem, smem, any_spec, any_spec, any_spec, any_spec],
             out_specs=(any_spec, any_spec),
             scratch_shapes=[
                 pltpu.VMEM((width, slots), BF16),
@@ -479,11 +483,9 @@
                 pltpu.VMEM((2, 2, tokens, slots), BF16),
                 pltpu.VMEM((2, 2, 4, pairs) + blk, BF16),
                 pltpu.VMEM((2, 4, pairs) + blk, BF16),
-                pltpu.VMEM((2, pairs, 16, width // 2), BF16),
-                pltpu.VMEM((2, pairs, 16, width // 2), BF16),
                 pltpu.VMEM((2, pairs) + blk, BF16),
                 pltpu.VMEM((2, pairs) + blk, BF16),
-                pltpu.VMEM((DIRECT,) + blk, BF16),
+                pltpu.VMEM((2, pairs) + blk, BF16),
                 pltpu.VMEM((2, pairs) + blk, BF16),
                 pltpu.VMEM((rows, slots), F32),
                 pltpu.VMEM((rows, slots), F32),
@@ -492,11 +494,10 @@
                 pltpu.VMEM((rows, slots), F32),
                 pltpu.VMEM((2, 4 * rows, width), BF16),
                 pltpu.VMEM((2, 4 * rows, F_BLOCK), BF16),
-                pltpu.VMEM((4 * rows, width), F32),
                 pltpu.VMEM((experts, 8, 4 * rows, width), BF16),
                 pltpu.VMEM((W_SLOTS, width, F_BLOCK), BF16),
                 pltpu.VMEM((W_SLOTS * F_BLOCK + max(F_BLOCK, TOK_SLOTS * tokens), width), BF16),
-                dma((TOK_SLOTS,)), dma((W_SLOTS,)), dma((O_SLOTS,)), dma((2,)), dma, dma((2,)), dma((2,)),
+                dma, dma((TOK_SLOTS,)), dma((W_SLOTS,)), dma((O_SLOTS,)), dma((2,)), dma, dma((2,)), dma((2,)),
                 dma, dma((2, pairs)), dma((2, 2)), dma((2, 2, pairs)), dma((2,)), dma((2, 2)), dma, dma, dma((experts + 1,)), dma((4, experts + 1)),
             ],
             compiler_params=pltpu.CompilerParams(

time: 81 us -> 79.3 us (0.979)
  Pallas kernels: 80.2 us -> 78.5 us
    pallas_call x1, Pallas kernels: 67.8 us -> 66.1 us  [shard_body(): pl.pallas_call(route_kernel, out_shape=(jax.ShapeDtypeStruct((rows, token...]
where the time goes in v4:
time: 79.3 us; the launch traced here: 79.1 us
  Pallas kernels  78.5 us (99%)
    pallas_call x1, Pallas kernels, shard_body(): pl.pallas_call(route_kernel, out_shape=(jax.ShapeDtypeStruct((rows, token...  66.1 us
    pallas_call x1, Pallas kernels, shard_body(): pl.pallas_call(combine_kernel, out_shape=jax.ShapeDtypeStruct(tok.shape,...  12.4 us

profile of v4, /device:TPU:113, one launch (start us, length us, event | category | flops | bytes accessed | tf_op | source)
XLA Modules:
  0.0 79.1 jit_solution(1421608086746962564)
XLA Ops:
  0.7 66.1 %route.1 = (bf16[16,512,128]{2,1,0:T(8,128)(2,1)}, bf16[4,8,64,1280]{3,2,1,0:T(8,128)(2,1)}) custom-call(s32[16]{0:T(128)} %lens.1, f32[1]{0:T(128)S(6)} %copy.7.gain, bf16[1280,128]{1,0:T(8,128)(2,1)} %phi.1, bf16[16,512,1280]{2,1,0:T(8,128)(2,1)} %tok.1, bf16[4,1280,5120]{2,1,0:T(8,128)(2,1)} %w_in.1, bf16[4,5120,1280]{2,1,0:T(8,128)(2,1)} %w_out.1), custom_call_target="tpu_custom_call" | custom-call | tf_op jit(solution)/shard_map/route/pallas_call | solution.py:471
  66.8 12.4 %combine.1 = bf16[16,512,1280]{2,1,0:T(8,128)(2,1)} custom-call(bf16[16,512,128]{2,1,0:T(8,128)(2,1)} %get-tuple-element.7.c_hbm, bf16[4,8,64,1280]{3,2,1,0:T(8,128)(2,1)} %get-tuple-element.8.y_hbm), custom_call_target="tpu_custom_call" | custom-call | tf_op jit(solution)/shard_map/combine/pallas_call | solution.py:508
